TPU v7x, 32 devices: a whole 2x2x4 slice. The times are simulated.
32 devices in a mesh: len: 2 (over x), wid: 4 (over z), dep: 4 (over y, core).
Axes of the slice: x: 2, y: 2, z: 4, core: 2. Of those that a mesh axis runs over, the one named last changes fastest.
Arguments:
- coords: float32 [3, 32768], P(None, ('len', 'wid', 'dep')), may hold values from -3 to 3
- velocity: float32 [3, 32768], P(None, ('len', 'wid', 'dep')), may hold values from -6 to 6
- node_mass: float32 [32768], P(('len', 'wid', 'dep')), may hold values from 0.5 to 2
- corner_nodes: int32 [4, 32768], P(None, ('len', 'wid', 'dep')), may hold values from 0 to 1151, as said below
- shape_grad: float32 [8, 32768], P(None, ('len', 'wid', 'dep')), may hold values from -5 to 5
- frame_angles: float32 [2, 32768], P(None, ('len', 'wid', 'dep')), may hold values from -3.140625 to 3.140625
- volume: float32 [32768], P(('len', 'wid', 'dep')), may hold values from 0.5 to 2
- stress: float32 [3, 32768], P(None, ('len', 'wid', 'dep')), may hold values from -5 to 5
- send_nodes: int32 [32, 16, 256], P(('len', 'wid', 'dep')), may hold values from 0 to 1023
- tile_count: int32 [32], P(('len', 'wid', 'dep')), may hold values from 1 to 4, as said below
- tile_nodes: int32 [128, 128], P(('len', 'wid', 'dep')), may hold values from 0 to 4095
- tile_facets: int32 [4, 128, 128], P(None, ('len', 'wid', 'dep')), may hold values from 0 to 4095
- pair_mask: int32 [128, 128, 128], P(('len', 'wid', 'dep')), may hold values 0 or 1
Outputs:
- coords_out: float32 [3, 32768], P(None, ('len', 'wid', 'dep'))
- velocity_out: float32 [3, 32768], P(None, ('len', 'wid', 'dep'))
- stress_out: float32 [3, 32768], P(None, ('len', 'wid', 'dep'))
Inputs may be any that keep to these rules, and one draw needn't show every extreme that they name: `corner_nodes`: for the element at device-local position i (i = e mod 1024), every entry lies from (i // 128) * 128 to (i // 128) * 128 + 2 * 128 - 1. An entry j below 1024 names the element device's own node j; an entry 1024 + i names node i of the next device in the order len, wid, dep, the last device's next being the first. `send_nodes`: entry [p, g, k] is a node of device p, by its local number, sent to device g of p's slab; nodes may repeat. `tile_count`: some device has 4 live tiles in every draw; a device's tiles at and past its count are not used. `tile_nodes`: slot g * 256 + k of the tile's device is slot k of what device g of its slab sends it. `tile_facets`: slots as for tile_nodes, one for each of a facet's four corners.
All inputs are finite; a program needn't handle non-finite values. No bound on the sum of `pair_mask` on one device may be relied on, other than what follows from the above.
Results may differ from a plain program's by a relative error of at most 0.0003.
Values sent between devices are 32-bit elements; how exact they have to be, the bound alone decides.
A program may use at most 64 MiB of HBM per device.

v0:
```python
import functools

import jax
import jax.numpy as jnp
from jax import lax
from jax.experimental import pallas as pl
from jax.experimental.pallas import tpu as pltpu
from jax.sharding import PartitionSpec as P

STEPS = 2
TIME_STEP = 0.1
YOUNG_MOD = 1.0
POISSON = 0.3
HOURGLASS = 0.1
RADIUS_SQ = 1.0
STIFFNESS = 0.1
DAMPING = 0.05

LANES = 128
MESH = pl.DeviceIdType.MESH
F32 = jnp.float32
BF16 = jnp.bfloat16


def two_parts(values):
    first = values.astype(BF16)
    return first, (values - first.astype(F32)).astype(BF16)


def lane_take(table, low):
    return jnp.take_along_axis(table, low, axis=1, mode="promise_in_bounds")


def nt_dot(left, right):
    return lax.dot_general(left, right, (((1,), (1,)), ((), ())), preferred_element_type=F32)


def nn_dot(left, right):
    return lax.dot_general(left, right, (((1,), (0,)), ((), ())), preferred_element_type=F32)


def kernel(
    sizes,
    coords_hbm, velocity_hbm, mass_hbm, corner_hbm, grad_hbm, angles_hbm, volume_hbm, stress_hbm,
    send_hbm, count_in, nodes_hbm, facets_hbm, mask_hbm,
    coords_out, velocity_out, stress_out,
    coords_in, velocity_in, mass_in, corner_in, grad_in, angles_in, volume_in, stress_in,
    send_in, nodes_in, facets_in, mask_in, in_sem,
    pos, vel, corner, grad, stress, angle, slot_high, tile_ids, win_hot, tile_hot, node_hot,
    win_rows, tile_lhs, node_lhs,
    send_buf, recv_buf, again_buf, fresh_buf, back_buf, answer_buf, ghost_send, ghost_recv, rim_send, rim_recv,
    out_send_sem, out_recv_sem, back_send_sem, back_recv_sem, edge_send_sem, edge_recv_sem,
):
    n_len, n_wid, n_dep = sizes
    group = n_wid * n_dep
    devices = n_len * group
    rows = coords_in.shape[1] // LANES
    order = sorted(range(1, group), key=lambda d: -min(d, group - d))
    halves = send_in.shape[2] // LANES
    tiles = nodes_in.shape[0]
    my_len = lax.axis_index("len")
    my_place = lax.axis_index("wid") * n_dep + lax.axis_index("dep")
    my_id = my_len * group + my_place

    def by_id(p):
        return (p // group, (p % group) // n_dep, p % n_dep)

    def partner(d):
        g = lax.rem(my_place + d, group)
        return g, (my_len, g // n_dep, lax.rem(g, n_dep))

    before = by_id(lax.rem(my_id + devices - 1, devices))
    after = by_id(lax.rem(my_id + 1, devices))

    loads = [
        pltpu.make_async_copy(src, dst, in_sem.at[n])
        for n, (src, dst) in enumerate((
            (coords_hbm, coords_in), (velocity_hbm, velocity_in), (send_hbm, send_in),
            (corner_hbm, corner_in), (stress_hbm, stress_in), (grad_hbm, grad_in),
            (angles_hbm, angles_in), (mass_hbm, mass_in), (volume_hbm, volume_in),
            (nodes_hbm, nodes_in), (facets_hbm, facets_in), (mask_hbm, mask_in),
        ))
    ]
    barrier = pltpu.get_barrier_semaphore()
    for d in order:
        pl.semaphore_signal(barrier, inc=1, device_id=partner(d)[1], device_id_type=MESH)
    pl.semaphore_signal(barrier, inc=1, device_id=before, device_id_type=MESH)
    pl.semaphore_signal(barrier, inc=1, device_id=after, device_id_type=MESH)

    for load in loads:
        load.start()
    for load in loads[:3]:
        load.wait()
    for i in range(rows):
        cols = pl.ds(i * LANES, LANES)
        pos[pl.ds(i, 3, stride=rows), :] = coords_in[:, cols]
        for k in range(3):
            vel[pl.ds(k * 2 * rows + i, 1), :] = velocity_in[pl.ds(k, 1), cols]

    def velocity_rows(k):
        return vel[pl.ds(k * 2 * rows, rows), :]

    def fill_ghosts(step):
        for k in range(3):
            ghost_send[step, pl.ds(k, 1), :] = vel[pl.ds(k * 2 * rows, 1), :]

    def fill_slots(step):
        tables = [velocity_rows(k) for k in range(3)]
        if step == 0:
            tables += [pos[pl.ds(k * rows, rows), :] for k in range(3)]
        for half in range(halves):
            ids = send_in[0, :, pl.ds(half * LANES, LANES)]
            low, high = ids & (LANES - 1), ids >> 7
            if step == 0:
                slot_high[:, half, :] = high
            for c, table in enumerate(tables):
                found = jnp.zeros(ids.shape, F32)
                for h in range(rows):
                    row = jnp.broadcast_to(table[h : h + 1], ids.shape)
                    found = jnp.where(high == h, lane_take(row, low), found)
                if step == 0:
                    send_buf[:, c * halves + half, :] = found
                else:
                    again_buf[step - 1, :, c * halves + half, :] = found

    fill_ghosts(0)
    fill_slots(0)
    for load in loads[3:]:
        load.wait()
    for i in range(rows):
        cols = pl.ds(i * LANES, LANES)
        stress[pl.ds(i, 3, stride=rows), :] = stress_in[:, cols]
        corner[pl.ds(i, 4, stride=rows), :] = corner_in[:, cols]
        grad[pl.ds(i, 8, stride=rows), :] = grad_in[:, cols]
        angle[pl.ds(i, 2, stride=rows), :] = angles_in[:, cols]
    tile_rows = tile_ids.shape[0]
    tile_ids[...] = jnp.zeros_like(tile_ids)
    tile_ids[pl.ds(0, tiles), :] = nodes_in[...]
    for a in range(4):
        tile_ids[pl.ds((a + 1) * tiles, tiles), :] = facets_in[a]

    def edge_copy(step, which):
        src, dst, target = ((ghost_send, ghost_recv, before), (rim_send, rim_recv, after))[which]
        return pltpu.make_async_remote_copy(
            src_ref=src.at[step], dst_ref=dst.at[step],
            send_sem=edge_send_sem.at[step, which], recv_sem=edge_recv_sem.at[step, which],
            device_id=target, device_id_type=MESH,
        )

    def group_copy(step, d, back):
        g, target = partner(d)
        if back:
            src, dst, ss, rs = back_buf.at[step], answer_buf.at[step], back_send_sem, back_recv_sem
        elif step == 0:
            src, dst, ss, rs = send_buf, recv_buf, out_send_sem, out_recv_sem
        else:
            src, dst, ss, rs = again_buf.at[step - 1], fresh_buf.at[step - 1], out_send_sem, out_recv_sem
        return pltpu.make_async_remote_copy(
            src_ref=src.at[g], dst_ref=dst.at[my_place],
            send_sem=ss.at[step, d - 1], recv_sem=rs.at[step, d - 1],
            device_id=target, device_id_type=MESH,
        )

    pl.semaphore_wait(barrier, group + 1)

    sub = lax.broadcasted_iota(jnp.int32, (LANES, LANES), 0)
    for step in range(STEPS):
        edge_copy(step, 0).start()
        for d in order:
            group_copy(step, d, False).start()
        if step == 0:
            recv_buf[my_place] = send_buf[my_place]
        else:
            fresh_buf[step - 1, my_place] = again_buf[step - 1, my_place]

        if step == 0:
            first_row = lax.broadcasted_iota(jnp.int32, (rows, LANES), 0) * LANES
            corner_low, corner_far = [], []
            for a in range(4):
                local = corner[pl.ds(a * rows, rows), :] - first_row
                corner_low.append(local & (LANES - 1))
                corner_far.append(local >= LANES)
                for i in range(rows):
                    hot = (sub == corner_low[a][i : i + 1]).astype(F32).astype(BF16)
                    win_hot[i, :, pl.ds(a * LANES, LANES)] = hot
            polar, azim = angle[pl.ds(0, rows), :], angle[pl.ds(rows, rows), :]
            cos_p, sin_p, cos_a, sin_a = jnp.cos(polar), jnp.sin(polar), jnp.cos(azim), jnp.sin(azim)
            one = (cos_p * cos_a, cos_p * sin_a, -sin_p)
            two = (-sin_a, cos_a)
            volume = volume_in[...]
            mass = mass_in[...]
            gx = [grad[pl.ds(a * rows, rows), :] for a in range(4)]
            gy = [grad[pl.ds((4 + a) * rows, rows), :] for a in range(4)]

        edge_copy(step, 0).wait_recv()
        for k in range(3):
            vel[pl.ds(k * 2 * rows + rows, 1), :] = ghost_recv[step, pl.ds(k, 1), :]
        corner_vel = []
        for k in range(3):
            near = velocity_rows(k)
            far = vel[pl.ds(k * 2 * rows + 1, rows), :]
            corner_vel.append([
                jnp.where(corner_far[a], lane_take(far, corner_low[a]), lane_take(near, corner_low[a]))
                for a in range(4)
            ])
        xx = yy = xy = jnp.zeros((rows, LANES), F32)
        for a in range(4):
            u = sum(one[k] * corner_vel[k][a] for k in range(3))
            w = sum(two[k] * corner_vel[k][a] for k in range(2))
            xx += gx[a] * u
            yy += gy[a] * w
            xy += gy[a] * u + gx[a] * w
        factor = TIME_STEP * YOUNG_MOD / (1.0 - POISSON * POISSON)
        sxx = stress[pl.ds(0, rows), :] + factor * (xx + POISSON * yy)
        syy = stress[pl.ds(rows, rows), :] + factor * (POISSON * xx + yy)
        sxy = stress[pl.ds(2 * rows, rows), :] + factor * 0.5 * (1.0 - POISSON) * xy
        stress[pl.ds(0, rows), :] = sxx
        stress[pl.ds(rows, rows), :] = syy
        stress[pl.ds(2 * rows, rows), :] = sxy
        hour = [
            HOURGLASS * volume
            * (corner_vel[k][0] - corner_vel[k][1] + corner_vel[k][2] - corner_vel[k][3])
            for k in range(3)
        ]
        for a in range(4):
            f1 = -volume * (gx[a] * sxx + gy[a] * sxy)
            f2 = -volume * (gy[a] * syy + gx[a] * sxy)
            for k in range(3):
                force = one[k] * f1 - (1.0 if a % 2 == 0 else -1.0) * hour[k]
                if k < 2:
                    force += two[k] * f2
                first = force.astype(BF16).astype(F32)
                for part, value in enumerate((first, force - first)):
                    for side in range(2):
                        keep = corner_far[a] if side else jnp.logical_not(corner_far[a])
                        win_rows[a, pl.ds(part * 8 + k * 2 + side, rows, stride=16), :] = jnp.where(
                            keep, value, 0.0
                        )
        for i in range(rows):
            left = jnp.concatenate(
                [win_rows[a, pl.ds(i * 16, 16), :].astype(BF16) for a in range(4)], axis=1
            )
            summed = nt_dot(left, win_hot[i])
            rim_send[step, pl.ds(i * 8, 8), :] = summed[:8] + summed[8:]
        edge = pltpu.make_async_remote_copy(
            src_ref=rim_send.at[step, pl.ds((rows - 1) * 8, 8)], dst_ref=rim_recv.at[step],
            send_sem=edge_send_sem.at[step, 1], recv_sem=edge_recv_sem.at[step, 1],
            device_id=after, device_id_type=MESH,
        )
        edge.start()

        if step == 0:
            for b in range(5 * tiles):
                low = tile_ids[pl.ds(b, 1), :] & (LANES - 1)
                tile_hot[:, pl.ds(b * LANES, LANES)] = (sub == low).astype(F32).astype(BF16)
            for g in range(group):
                for half in range(halves):
                    low = send_in[0, pl.ds(g, 1), pl.ds(half * LANES, LANES)] & (LANES - 1)
                    node_hot[:, pl.ds((g * halves + half) * LANES, LANES)] = (
                        (sub == low).astype(F32).astype(BF16)
                    )
            ids = tile_ids[...]
            ids_low, ids_high = ids & (LANES - 1), ids >> 7

        landed = recv_buf if step == 0 else fresh_buf.at[step - 1]
        found = [jnp.zeros(ids.shape, F32) for c in range(6 if step == 0 else 3)]
        for d in order[::-1]:
            group_copy(step, d, False).wait_recv()
        for g in range(group):
            for half in range(halves):
                match = ids_high == g * halves + half
                for c in range(len(found)):
                    row = jnp.broadcast_to(landed[g, pl.ds(c * halves + half, 1), :], ids.shape)
                    found[c] = jnp.where(match, lane_take(row, ids_low), found[c])
        if step == 0:
            slot_pos = found[3:]
        else:
            slot_pos = [slot_pos[k] + TIME_STEP * found[k] for k in range(3)]
        state = slot_pos + found[:3]
        centre = [
            0.25 * sum(s[(a + 1) * tiles : (a + 2) * tiles] for a in range(4)) for s in state
        ]
        nodes = [s[:tiles] for s in state]
        node_mix = [STIFFNESS * nodes[k] - DAMPING * nodes[3 + k] for k in range(3)]
        facet_mix = [STIFFNESS * centre[k] - DAMPING * centre[3 + k] for k in range(3)]
        lead = jnp.concatenate(nodes[:3] + [jnp.zeros((16 - 3 * tiles % 16, LANES), F32)], axis=0)
        columns = jnp.transpose(lead)
        ones = jnp.ones((1, LANES), F32)
        blank = jnp.zeros((4, LANES), F32)
        node_force = [[None] * tiles for k in range(3)]
        facet_force = [[None] * tiles for k in range(3)]
        for t in range(tiles):
            live = jnp.where(t < count_in[0], 1.0, 0.0)
            dist = jnp.zeros((LANES, LANES), F32)
            for k in range(3):
                gap = columns[:, k * tiles + t : k * tiles + t + 1] - centre[k][t : t + 1]
                dist += gap * gap
            weight = mask_in[t].astype(F32) * (live * jnp.maximum(RADIUS_SQ - dist, 0.0))
            w1, w2 = two_parts(weight)
            a1, a2 = two_parts(jnp.concatenate([m[t : t + 1] for m in node_mix] + [ones, blank], axis=0))
            b1, b2 = two_parts(jnp.concatenate([m[t : t + 1] for m in facet_mix] + [ones, blank], axis=0))
            left_a = jnp.concatenate([a1, a2], axis=0)
            left_b = jnp.concatenate([b1, b2], axis=0)
            to_facet = nn_dot(
                jnp.concatenate([left_a, left_a], axis=1), jnp.concatenate([w1, w2], axis=0)
            )
            to_node = nt_dot(
                jnp.concatenate([left_b, left_b], axis=1), jnp.concatenate([w1, w2], axis=1)
            )
            to_facet = to_facet[:8] + to_facet[8:]
            to_node = to_node[:8] + to_node[8:]
            for k in range(3):
                node_force[k][t] = node_mix[k][t : t + 1] * to_node[3:4] - to_node[k : k + 1]
                facet_force[k][t] = -0.25 * (
                    to_facet[k : k + 1] - to_facet[3:4] * facet_mix[k][t : t + 1]
                )
        spans = halves * group
        high_iota = lax.broadcasted_iota(jnp.int32, (spans, LANES), 0)
        for b in range(5 * tiles):
            high = ids_high[b : b + 1]
            match = high_iota == (high % halves) * group + high // halves
            for k in range(3):
                row = node_force[k][b] if b < tiles else facet_force[k][b % tiles]
                chosen = jnp.where(match, jnp.broadcast_to(row, match.shape), 0.0)
                p1, p2 = two_parts(chosen)
                cols = pl.ds(b * LANES, LANES)
                tile_lhs[pl.ds(k * spans, spans), cols] = p1
                tile_lhs[pl.ds((3 + k) * spans, spans), cols] = p2
        slots = nt_dot(tile_lhs[...], tile_hot[...])
        slots = slots[: 3 * spans] + slots[3 * spans :]
        for r in range(3 * halves):
            back_buf[step, :, r, :] = slots[r * group : (r + 1) * group]
        for d in order:
            group_copy(step, d, True).start()
        answer_buf[step, my_place] = back_buf[step, my_place]
        edge.wait_recv()
        internal = []
        for k in range(3):
            near = rim_send[step, pl.ds(k * 2, rows, stride=8), :]
            far = rim_send[step, pl.ds(k * 2 + 1, rows - 1, stride=8), :]
            edge_row = rim_recv[step, pl.ds(k * 2 + 1, 1), :]
            internal.append(near + jnp.concatenate([edge_row, far], axis=0))
        row_iota = lax.broadcasted_iota(jnp.int32, (rows, LANES), 0)
        for d in order[::-1]:
            group_copy(step, d, True).wait_recv()
        for g in range(group):
            for half in range(halves):
                high = slot_high[g, pl.ds(half, 1), :]
                match = row_iota == high
                chosen = jnp.concatenate([
                    jnp.where(
                        match,
                        jnp.broadcast_to(answer_buf[step, g, pl.ds(k * halves + half, 1), :], match.shape),
                        0.0,
                    )
                    for k in range(3)
                ], axis=0)
                first = chosen.astype(BF16).astype(F32)
                both = jnp.concatenate([first, chosen - first], axis=0).astype(BF16)
                node_lhs[:, pl.ds((g * halves + half) * LANES, LANES)] = both
        contact = nt_dot(node_lhs[...], node_hot[...])
        contact = contact[: 3 * rows] + contact[3 * rows :]
        for k in range(3):
            fresh = velocity_rows(k) + TIME_STEP * (
                internal[k] + contact[k * rows : (k + 1) * rows]
            ) / mass
            vel[pl.ds(k * 2 * rows, rows), :] = fresh
            pos[pl.ds(k * rows, rows), :] = pos[pl.ds(k * rows, rows), :] + TIME_STEP * fresh
        if step + 1 < STEPS:
            fill_ghosts(step + 1)
            fill_slots(step + 1)

    coords_out[...] = pos[...]
    for k in range(3):
        velocity_out[pl.ds(k * rows, rows), :] = velocity_rows(k)
    stress_out[...] = stress[...]
    for step in range(STEPS):
        edge_copy(step, 0).wait_send()
        pltpu.make_async_remote_copy(
            src_ref=rim_send.at[step, pl.ds((rows - 1) * 8, 8)], dst_ref=rim_recv.at[step],
            send_sem=edge_send_sem.at[step, 1], recv_sem=edge_recv_sem.at[step, 1],
            device_id=after, device_id_type=MESH,
        ).wait_send()
        for d in range(1, group):
            group_copy(step, d, False).wait_send()
            group_copy(step, d, True).wait_send()


def arrange(coords_rows, velocity_rows, stress_rows, coords_out, velocity_out, stress_out):
    rows = coords_rows.shape[0] // 3
    pairs = ((coords_rows, coords_out), (velocity_rows, velocity_out), (stress_rows, stress_out))
    for source, target in pairs:
        for i in range(rows):
            target[:, pl.ds(i * LANES, LANES)] = source[pl.ds(i, 3, stride=rows), :]


def per_device(
    sizes, coords, velocity, node_mass, corner_nodes, shape_grad, frame_angles, volume, stress,
    send_nodes, tile_count, tile_nodes, tile_facets, pair_mask,
):
    count = coords.shape[1]
    rows = count // LANES
    group = sizes[1] * sizes[2]
    cap = send_nodes.shape[2]
    tiles = tile_nodes.shape[0]
    spans = group * cap // LANES
    vmem = pl.BlockSpec(memory_space=pltpu.VMEM)
    smem = pl.BlockSpec(memory_space=pltpu.SMEM)
    state = jax.ShapeDtypeStruct((3, count), F32)
    packed = jax.ShapeDtypeStruct((3 * rows, LANES), F32)
    hbm = pl.BlockSpec(memory_space=pl.ANY)
    halves = cap // LANES
    arrays = (
        coords, velocity, node_mass.reshape(rows, LANES), corner_nodes, shape_grad, frame_angles,
        volume.reshape(rows, LANES), stress, send_nodes, tile_nodes, tile_facets, pair_mask,
    )
    dma = pltpu.SemaphoreType.DMA
    finals = pl.pallas_call(
        functools.partial(kernel, sizes),
        out_shape=(packed, packed, packed),
        in_specs=[hbm] * 9 + [smem] + [hbm] * 3,
        out_specs=(vmem, vmem, vmem),
        scratch_shapes=[pltpu.VMEM(a.shape, a.dtype) for a in arrays] + [
            dma((len(arrays),)),
            pltpu.VMEM((3 * rows, LANES), F32),
            pltpu.VMEM((6 * rows, LANES), F32),
            pltpu.VMEM((4 * rows, LANES), jnp.int32),
            pltpu.VMEM((8 * rows, LANES), F32),
            pltpu.VMEM((3 * rows, LANES), F32),
            pltpu.VMEM((2 * rows, LANES), F32),
            pltpu.VMEM((group, halves, LANES), jnp.int32),
            pltpu.VMEM((-(-5 * tiles // 8) * 8, LANES), jnp.int32),
            pltpu.VMEM((rows, LANES, 4 * LANES), BF16),
            pltpu.VMEM((LANES, 5 * tiles * LANES), BF16),
            pltpu.VMEM((LANES, group * cap), BF16),
            pltpu.VMEM((4, 16 * rows, LANES), F32),
            pltpu.VMEM((6 * spans, 5 * tiles * LANES), BF16),
            pltpu.VMEM((6 * rows, group * cap), BF16),
            pltpu.VMEM((group, 6 * halves, LANES), F32),
            pltpu.VMEM((group, 6 * halves, LANES), F32),
            pltpu.VMEM((STEPS - 1, group, 3 * halves, LANES), F32),
            pltpu.VMEM((STEPS - 1, group, 3 * halves, LANES), F32),
            pltpu.VMEM((STEPS, group, 3 * halves, LANES), F32),
            pltpu.VMEM((STEPS, group, 3 * halves, LANES), F32),
            pltpu.VMEM((STEPS, 3, LANES), F32),
            pltpu.VMEM((STEPS, 3, LANES), F32),
            pltpu.VMEM((STEPS, 8 * rows, LANES), F32),
            pltpu.VMEM((STEPS, 8, LANES), F32),
            dma((STEPS, group - 1)),
            dma((STEPS, group - 1)),
            dma((STEPS, group - 1)),
            dma((STEPS, group - 1)),
            dma((STEPS, 2)),
            dma((STEPS, 2)),
        ],
        compiler_params=pltpu.CompilerParams(collective_id=0, has_side_effects=True),
    )(*arrays[:9], tile_count, *arrays[9:])
    return pl.pallas_call(
        arrange,
        out_shape=(state, state, state),
        in_specs=[vmem] * 3,
        out_specs=(vmem, vmem, vmem),
    )(*finals)


def solution(mesh):
    axes = ("len", "wid", "dep")
    flat, wide = P(axes), P(None, axes)
    sizes = tuple(mesh.shape[name] for name in axes)
    return jax.shard_map(
        functools.partial(per_device, sizes),
        mesh=mesh,
        in_specs=(
            wide, wide, flat, wide, wide, wide, flat, wide,
            P(axes, None, None), flat, P(axes, None), P(None, axes, None), P(axes, None, None),
        ),
        out_specs=(wide, wide, wide),
        check_vma=False,
    )
```

profile of v0, /device:TPU:0, one launch (start us, length us, event | category | flops | bytes accessed | tf_op | source)
XLA Modules:
  0.0 35.1 jit_solution(4337531845070685619)
XLA Ops:
  1.3 32.5 %shard_map.148 = (f32[24,128]{1,0:T(8,128)}, f32[24,128]{1,0:T(8,128)}, f32[24,128]{1,0:T(8,128)}) custom-call(f32[3,1024]{1,0:T(4,128)} %coords_hbm.1, f32[3,1024]{1,0:T(4,128)} %velocity_hbm.1, f32[8,128]{1,0:T(8,128)} %bitcast.2, s32[4,1024]{1,0:T(4,128)} %corner_hbm.1, f32[8,1024]{1,0:T(8,128)} %grad_hbm.1, f32[2,1024]{1,0:T(2,128)} %angles_hbm.1, ...), custom_call_target="tpu_custom_call" | custom-call | tf_op jit(solution)/shard_map/pallas_call | solution.py:418
  33.8 1.4 %shard_map.149 = (f32[3,1024]{1,0:T(4,128)}, f32[3,1024]{1,0:T(4,128)}, f32[3,1024]{1,0:T(4,128)}) custom-call(f32[24,128]{1,0:T(8,128)} %get-tuple-element.6.coords_rows, f32[24,128]{1,0:T(8,128)} %get-tuple-element.7.velocity_rows, f32[24,128]{1,0:T(8,128)} %get-tuple-element.8.stress_rows), custom_call_target="tpu_custom_call" | custom-call | tf_op jit(solution)/shard_map/pallas_call | solution.py:458
where the time goes:
time: 35.4 us; the launch traced here: 35.1 us
  Pallas kernels  33.8 us (95%)
  between operations  1.29 us (4%)
    pallas_call x1, Pallas kernels, per_device(): pl.pallas_call(functools.partial(kernel, sizes), out_shape=(packed, packe...  32.5 us
    pallas_call x1, Pallas kernels, per_device(): pl.pallas_call(arrange, out_shape=(state, state, state), in_specs=[vmem]...  1.37 us

commit v1 on v0

v1 whole, which is shorter than its diff:
```python
import functools

import jax
import jax.numpy as jnp
from jax import lax
from jax.experimental import pallas as pl
from jax.experimental.pallas import tpu as pltpu
from jax.sharding import PartitionSpec as P

STEPS = 2
TIME_STEP = 0.1
YOUNG_MOD = 1.0
POISSON = 0.3
HOURGLASS = 0.1
RADIUS_SQ = 1.0
STIFFNESS = 0.1
DAMPING = 0.05

LANES = 128
MESH = pl.DeviceIdType.MESH
F32 = jnp.float32
BF16 = jnp.bfloat16


def two_parts(values):
    first = values.astype(BF16)
    return first, (values - first.astype(F32)).astype(BF16)


def lane_take(table, low):
    return jnp.take_along_axis(table, low, axis=1, mode="promise_in_bounds")


def nt_dot(left, right):
    return lax.dot_general(left, right, (((1,), (1,)), ((), ())), preferred_element_type=F32)


def nn_dot(left, right):
    return lax.dot_general(left, right, (((1,), (0,)), ((), ())), preferred_element_type=F32)


def kernel(
    sizes,
    coords_hbm, velocity_hbm, mass_hbm, corner_hbm, grad_hbm, angles_hbm, volume_hbm, stress_hbm,
    send_hbm, nodes_hbm, facets_hbm, mask_hbm, count_in,
    coords_out, velocity_out, stress_out,
    coords_in, velocity_in, mass_in, corner_in, grad_in, angles_in, volume_in, stress_in,
    send_in, nodes_in, facets_in, mask_in, in_sem,
    pos, vel, corner, grad, stress, angle, slot_ids, tile_ids, win_hot, tile_hot, node_hot,
    win_rows, force_rows, tile_lhs, node_lhs,
    send_buf, recv_buf, again_buf, fresh_buf, back_buf, answer_buf,
    first_buf, last_buf, ghost_recv, last_recv,
    corner_prev, grad_prev, angles_prev, volume_prev, stress_prev,
    out_send_sem, out_recv_sem, back_send_sem, back_recv_sem, edge_send_sem, edge_recv_sem,
    prev_send_sem, prev_recv_sem,
):
    n_len, n_wid, n_dep = sizes
    group = n_wid * n_dep
    devices = n_len * group
    rows = coords_in.shape[1] // LANES
    halves = send_in.shape[2] // LANES
    tiles = nodes_in.shape[0]
    my_len = lax.axis_index("len")
    my_wid = lax.axis_index("wid")
    my_dep = lax.axis_index("dep")
    my_place = my_wid * n_dep + my_dep
    my_id = my_len * group + my_place

    def by_id(p):
        return (p // group, (p % group) // n_dep, p % n_dep)

    upper = (2 * my_wid) // n_wid
    shifts = sorted(range(1, n_dep), key=lambda d: -min(d, n_dep - d))
    peers = []
    for r in range(n_wid):
        across = r + (1 - upper) * (n_wid - 1 - 2 * r)
        for shift in shifts:
            peers.append((across, lax.rem(my_dep + shift, n_dep)))
        if r < n_wid - 1:
            up = r + (r - my_wid + n_wid) // n_wid
            down = n_wid - 1 - r - (my_wid - (n_wid - 1 - r) + n_wid) // n_wid
            peers.append((upper * up + (1 - upper) * down, my_dep))
    places = [wid * n_dep + dep for wid, dep in peers]
    count = group - 1
    arrival = [my_place] + places[::-1]

    before = by_id(lax.rem(my_id + devices - 1, devices))
    after = by_id(lax.rem(my_id + 1, devices))

    loads = [
        pltpu.make_async_copy(src, dst, in_sem.at[n])
        for n, (src, dst) in enumerate((
            (send_hbm, send_in), (velocity_hbm, velocity_in), (coords_hbm, coords_in),
            (corner_hbm, corner_in), (stress_hbm, stress_in), (grad_hbm, grad_in),
            (angles_hbm, angles_in), (mass_hbm, mass_in), (volume_hbm, volume_in),
            (nodes_hbm, nodes_in), (facets_hbm, facets_in), (mask_hbm, mask_in),
        ))
    ]
    for load in loads[:3]:
        load.start()
    barrier = pltpu.get_barrier_semaphore()
    for wid, dep in peers:
        pl.semaphore_signal(barrier, inc=1, device_id=(my_len, wid, dep), device_id_type=MESH)
    pl.semaphore_signal(barrier, inc=1, device_id=before, device_id_type=MESH)
    pl.semaphore_signal(barrier, inc=1, device_id=after, device_id_type=MESH)
    for load in loads[3:]:
        load.start()
    for load in loads[:3]:
        load.wait()
    for i in range(rows):
        cols = pl.ds(i * LANES, LANES)
        pos[pl.ds(i, 3, stride=rows), :] = coords_in[:, cols]
        for k in range(3):
            vel[pl.ds(k * 2 * rows + i, 1), :] = velocity_in[pl.ds(k, 1), cols]

    def velocity_rows(k):
        return vel[pl.ds(k * 2 * rows, rows), :]

    def fill_edges(step):
        for k in range(3):
            first_buf[step - 1, pl.ds(k, 1), :] = vel[pl.ds(k * 2 * rows, 1), :]
            last_buf[step - 1, pl.ds(k, 1), :] = vel[pl.ds(k * 2 * rows + rows - 1, 1), :]

    def fill_slots(step):
        tables = [velocity_rows(k) for k in range(3)]
        if step == 0:
            tables += [pos[pl.ds(k * rows, rows), :] for k in range(3)]
        for half in range(halves):
            ids = send_in[0, :, pl.ds(half * LANES, LANES)]
            low, high = ids & (LANES - 1), ids >> 7
            if step == 0:
                slot_ids[:, half, :] = ids
            for c, table in enumerate(tables):
                found = jnp.zeros(ids.shape, F32)
                for h in range(rows):
                    row = jnp.broadcast_to(table[h : h + 1], ids.shape)
                    found = jnp.where(high == h, lane_take(row, low), found)
                if step == 0:
                    send_buf[:, c * halves + half, :] = found
                else:
                    again_buf[step - 1, :, c * halves + half, :] = found

    def remote(src, dst, send_sem, recv_sem, target):
        return pltpu.make_async_remote_copy(
            src_ref=src, dst_ref=dst, send_sem=send_sem, recv_sem=recv_sem,
            device_id=target, device_id_type=MESH,
        )

    final = pl.ds((rows - 1) * LANES, LANES)

    def edge_copies(step):
        if step == 0:
            first, last = velocity_in.at[:, pl.ds(0, LANES)], velocity_in.at[:, final]
        else:
            first, last = first_buf.at[step - 1], last_buf.at[step - 1]
        return (
            remote(first, ghost_recv.at[step], edge_send_sem.at[step, 0], edge_recv_sem.at[step, 0], before),
            remote(last, last_recv.at[step], edge_send_sem.at[step, 1], edge_recv_sem.at[step, 1], after),
        )

    def prev_copies():
        pairs = (
            (corner_in.at[:, final], corner_prev), (grad_in.at[:, final], grad_prev),
            (angles_in.at[:, final], angles_prev), (stress_in.at[:, final], stress_prev),
            (volume_in.at[pl.ds(rows - 1, 1), :], volume_prev),
        )
        return [
            remote(src, dst, prev_send_sem.at[n], prev_recv_sem.at[n], after)
            for n, (src, dst) in enumerate(pairs)
        ]

    def group_copy(step, j, back):
        wid, dep = peers[j]
        place = places[j]
        if back:
            src, dst, ss, rs = back_buf.at[step], answer_buf.at[step], back_send_sem, back_recv_sem
        elif step == 0:
            src, dst, ss, rs = send_buf, recv_buf, out_send_sem, out_recv_sem
        else:
            src, dst, ss, rs = again_buf.at[step - 1], fresh_buf.at[step - 1], out_send_sem, out_recv_sem
        return remote(
            src.at[place], dst.at[my_place], ss.at[step, j], rs.at[step, my_place], (my_len, wid, dep)
        )

    def group_arrival(step, j, back):
        wid, dep = peers[j]
        place = places[j]
        if back:
            src, dst, ss, rs = back_buf.at[step], answer_buf.at[step], back_send_sem, back_recv_sem
        elif step == 0:
            src, dst, ss, rs = send_buf, recv_buf, out_send_sem, out_recv_sem
        else:
            src, dst, ss, rs = again_buf.at[step - 1], fresh_buf.at[step - 1], out_send_sem, out_recv_sem
        return remote(
            src.at[place], dst.at[place], ss.at[step, j], rs.at[step, place], (my_len, wid, dep)
        )

    fill_slots(0)
    pl.semaphore_wait(barrier, group + 1)

    sub = lax.broadcasted_iota(jnp.int32, (LANES, LANES), 0)
    for step in range(STEPS):
        for j in range(count):
            group_copy(step, j, False).start()
        for copy in edge_copies(step):
            copy.start()

        if step == 0:
            for load in loads[3:]:
                load.wait()
            for copy in prev_copies():
                copy.start()
            for i in range(rows):
                cols = pl.ds(i * LANES, LANES)
                stress[pl.ds(i, 3, stride=rows), :] = stress_in[:, cols]
                corner[pl.ds(i, 4, stride=rows), :] = corner_in[:, cols]
                grad[pl.ds(i, 8, stride=rows), :] = grad_in[:, cols]
                angle[pl.ds(i, 2, stride=rows), :] = angles_in[:, cols]
            tile_ids[...] = jnp.zeros_like(tile_ids)
            tile_ids[pl.ds(0, tiles), :] = nodes_in[...]
            for a in range(4):
                tile_ids[pl.ds((a + 1) * tiles, tiles), :] = facets_in[a]
            first_row = lax.broadcasted_iota(jnp.int32, (rows, LANES), 0) * LANES
            corner_low, corner_far = [], []
            for a in range(4):
                local = corner[pl.ds(a * rows, rows), :] - first_row
                corner_low.append(local & (LANES - 1))
                corner_far.append(local >= LANES)
                for i in range(rows):
                    hot = (sub == corner_low[a][i : i + 1]).astype(F32).astype(BF16)
                    win_hot[i, :, pl.ds(a * LANES, LANES)] = hot
            polar, azim = angle[pl.ds(0, rows), :], angle[pl.ds(rows, rows), :]

            def frame(polar, azim):
                cos_p, sin_p, cos_a, sin_a = jnp.cos(polar), jnp.sin(polar), jnp.cos(azim), jnp.sin(azim)
                return (cos_p * cos_a, cos_p * sin_a, -sin_p), (-sin_a, cos_a)

            volume = volume_in[...]
            mass = mass_in[...]
            gx = [grad[pl.ds(a * rows, rows), :] for a in range(4)]
            gy = [grad[pl.ds((4 + a) * rows, rows), :] for a in range(4)]
            own = (frame(polar, azim), volume, gx, gy, corner_low, corner_far)
            for b in range(5 * tiles):
                low = tile_ids[pl.ds(b, 1), :] & (LANES - 1)
                tile_hot[:, pl.ds(b * LANES, LANES)] = (sub == low).astype(F32).astype(BF16)
            for n, g in enumerate(arrival):
                for half in range(halves):
                    low = slot_ids[g, pl.ds(half, 1), :] & (LANES - 1)
                    node_hot[:, pl.ds((n * halves + half) * LANES, LANES)] = (
                        (sub == low).astype(F32).astype(BF16)
                    )
            ids = tile_ids[...]
            ids_low, ids_high = ids & (LANES - 1), ids >> 7

        mine = send_buf if step == 0 else again_buf.at[step - 1]
        landed = recv_buf if step == 0 else fresh_buf.at[step - 1]
        found = [jnp.zeros(ids.shape, F32) for c in range(6 if step == 0 else 3)]
        for n, g in enumerate(arrival):
            if n:
                group_arrival(step, count - n, False).wait_recv()
            source = landed if n else mine
            for half in range(halves):
                match = ids_high == g * halves + half
                for c in range(len(found)):
                    row = jnp.broadcast_to(source[g, pl.ds(c * halves + half, 1), :], ids.shape)
                    found[c] = jnp.where(match, lane_take(row, ids_low), found[c])
        if step == 0:
            slot_pos = found[3:]
        else:
            slot_pos = [slot_pos[k] + TIME_STEP * found[k] for k in range(3)]
        state = slot_pos + found[:3]
        centre = [
            0.25 * sum(s[(a + 1) * tiles : (a + 2) * tiles] for a in range(4)) for s in state
        ]
        nodes = [s[:tiles] for s in state]
        node_mix = [STIFFNESS * nodes[k] - DAMPING * nodes[3 + k] for k in range(3)]
        facet_mix = [STIFFNESS * centre[k] - DAMPING * centre[3 + k] for k in range(3)]
        lead = jnp.concatenate(nodes[:3] + [jnp.zeros((16 - 3 * tiles % 16, LANES), F32)], axis=0)
        columns = jnp.transpose(lead)
        ones = jnp.ones((1, LANES), F32)
        blank = jnp.zeros((4, LANES), F32)
        node_force = [[None] * tiles for k in range(3)]
        facet_force = [[None] * tiles for k in range(3)]
        for t in range(tiles):
            live = jnp.where(t < count_in[0], 1.0, 0.0)
            dist = jnp.zeros((LANES, LANES), F32)
            for k in range(3):
                gap = columns[:, k * tiles + t : k * tiles + t + 1] - centre[k][t : t + 1]
                dist += gap * gap
            weight = mask_in[t].astype(F32) * (live * jnp.maximum(RADIUS_SQ - dist, 0.0))
            w1, w2 = two_parts(weight)
            a1, a2 = two_parts(jnp.concatenate([m[t : t + 1] for m in node_mix] + [ones, blank], axis=0))
            b1, b2 = two_parts(jnp.concatenate([m[t : t + 1] for m in facet_mix] + [ones, blank], axis=0))
            left_a = jnp.concatenate([a1, a2], axis=0)
            left_b = jnp.concatenate([b1, b2], axis=0)
            to_facet = nn_dot(
                jnp.concatenate([left_a, left_a], axis=1), jnp.concatenate([w1, w2], axis=0)
            )
            to_node = nt_dot(
                jnp.concatenate([left_b, left_b], axis=1), jnp.concatenate([w1, w2], axis=1)
            )
            to_facet = to_facet[:8] + to_facet[8:]
            to_node = to_node[:8] + to_node[8:]
            for k in range(3):
                node_force[k][t] = node_mix[k][t : t + 1] * to_node[3:4] - to_node[k : k + 1]
                facet_force[k][t] = -0.25 * (
                    to_facet[k : k + 1] - to_facet[3:4] * facet_mix[k][t : t + 1]
                )
        spans = halves * group
        high_iota = lax.broadcasted_iota(jnp.int32, (spans, LANES), 0)
        for b in range(5 * tiles):
            high = ids_high[b : b + 1]
            match = high_iota == (high % halves) * group + high // halves
            for k in range(3):
                row = node_force[k][b] if b < tiles else facet_force[k][b % tiles]
                chosen = jnp.where(match, jnp.broadcast_to(row, match.shape), 0.0)
                p1, p2 = two_parts(chosen)
                cols = pl.ds(b * LANES, LANES)
                tile_lhs[pl.ds(k * spans, spans), cols] = p1
                tile_lhs[pl.ds((3 + k) * spans, spans), cols] = p2
        slots = nt_dot(tile_lhs[...], tile_hot[...])
        slots = slots[: 3 * spans] + slots[3 * spans :]
        for r in range(3 * halves):
            back_buf[step, :, r, :] = slots[r * group : (r + 1) * group]
        for j in range(count):
            group_copy(step, j, True).start()

        if step == 0:
            for copy in prev_copies():
                copy.wait_recv()

            def whole(row):
                return jnp.broadcast_to(row, (8, LANES))

            prev_low, prev_far = [], []
            for a in range(4):
                local = corner_prev[pl.ds(a, 1), :] - (rows - 1) * LANES
                low = local & (LANES - 1)
                win_hot[rows, :, pl.ds(a * LANES, LANES)] = (sub == low).astype(F32).astype(BF16)
                prev_low.append(whole(low))
                prev_far.append(whole(local) >= LANES)
            prev = (
                frame(whole(angles_prev[pl.ds(0, 1), :]), whole(angles_prev[pl.ds(1, 1), :])),
                whole(volume_prev[...]),
                [whole(grad_prev[pl.ds(a, 1), :]) for a in range(4)],
                [whole(grad_prev[pl.ds(4 + a, 1), :]) for a in range(4)],
                prev_low, prev_far,
            )
            own_stress = [stress[pl.ds(k * rows, rows), :] for k in range(3)]
            prev_stress = [whole(stress_prev[pl.ds(k, 1), :]) for k in range(3)]

        def element_forces(batch, tension, near, far):
            (one, two), volume, gx, gy, low, beyond = batch
            corner_vel = [
                [
                    jnp.where(beyond[a], lane_take(far[k], low[a]), lane_take(near[k], low[a]))
                    for a in range(4)
                ]
                for k in range(3)
            ]
            xx = yy = xy = jnp.zeros(volume.shape, F32)
            for a in range(4):
                u = sum(one[k] * corner_vel[k][a] for k in range(3))
                w = sum(two[k] * corner_vel[k][a] for k in range(2))
                xx += gx[a] * u
                yy += gy[a] * w
                xy += gy[a] * u + gx[a] * w
            factor = TIME_STEP * YOUNG_MOD / (1.0 - POISSON * POISSON)
            sxx = tension[0] + factor * (xx + POISSON * yy)
            syy = tension[1] + factor * (POISSON * xx + yy)
            sxy = tension[2] + factor * 0.5 * (1.0 - POISSON) * xy
            hour = [
                HOURGLASS * volume
                * (corner_vel[k][0] - corner_vel[k][1] + corner_vel[k][2] - corner_vel[k][3])
                for k in range(3)
            ]
            forces = []
            for a in range(4):
                f1 = -volume * (gx[a] * sxx + gy[a] * sxy)
                f2 = -volume * (gy[a] * syy + gx[a] * sxy)
                parts = []
                for k in range(3):
                    force = one[k] * f1 - (1.0 if a % 2 == 0 else -1.0) * hour[k]
                    if k < 2:
                        force += two[k] * f2
                    first = force.astype(BF16).astype(F32)
                    parts.append((first, force - first))
                forces.append(parts)
            return [sxx, syy, sxy], forces

        for copy in edge_copies(step):
            copy.wait_recv()
        for k in range(3):
            vel[pl.ds(k * 2 * rows + rows, 1), :] = ghost_recv[step, pl.ds(k, 1), :]
        own_stress, forces = element_forces(
            own, own_stress,
            [velocity_rows(k) for k in range(3)],
            [vel[pl.ds(k * 2 * rows + 1, rows), :] for k in range(3)],
        )
        prev_stress, prev_forces = element_forces(
            prev, prev_stress,
            [whole(last_recv[step, pl.ds(k, 1), :]) for k in range(3)],
            [whole(vel[pl.ds(k * 2 * rows, 1), :]) for k in range(3)],
        )
        for a in range(4):
            for k in range(3):
                for part in range(2):
                    for side in range(2):
                        at = part * 8 + k * 2 + side
                        keep = corner_far[a] if side else jnp.logical_not(corner_far[a])
                        win_rows[a, pl.ds(at, rows, stride=16), :] = jnp.where(
                            keep, forces[a][k][part], 0.0
                        )
                        far_row = jnp.where(prev_far[a], prev_forces[a][k][part], 0.0)[:1]
                        win_rows[a, pl.ds(rows * 16 + at, 1), :] = far_row
        for i in range(rows + 1):
            left = jnp.concatenate(
                [win_rows[a, pl.ds(i * 16, 16), :].astype(BF16) for a in range(4)], axis=1
            )
            summed = nt_dot(left, win_hot[i])
            force_rows[pl.ds(i * 8, 8), :] = summed[:8] + summed[8:]
        internal = []
        for k in range(3):
            near = force_rows[pl.ds(k * 2, rows, stride=8), :]
            far = force_rows[pl.ds(k * 2 + 1, rows - 1, stride=8), :]
            edge_row = force_rows[pl.ds(rows * 8 + k * 2 + 1, 1), :]
            internal.append(near + jnp.concatenate([edge_row, far], axis=0))
        if step + 1 == STEPS:
            for k in range(3):
                for i in range(rows):
                    stress_out[pl.ds(k, 1), pl.ds(i * LANES, LANES)] = own_stress[k][i : i + 1]
        row_iota = lax.broadcasted_iota(jnp.int32, (rows, LANES), 0)
        for n, g in enumerate(arrival):
            if n:
                group_arrival(step, count - n, True).wait_recv()
            source = answer_buf if n else back_buf
            for half in range(halves):
                high = slot_ids[g, pl.ds(half, 1), :] >> 7
                match = row_iota == high
                chosen = jnp.concatenate([
                    jnp.where(
                        match,
                        jnp.broadcast_to(source[step, g, pl.ds(k * halves + half, 1), :], match.shape),
                        0.0,
                    )
                    for k in range(3)
                ], axis=0)
                first = chosen.astype(BF16).astype(F32)
                both = jnp.concatenate([first, chosen - first], axis=0).astype(BF16)
                node_lhs[:, pl.ds((n * halves + half) * LANES, LANES)] = both
        contact = nt_dot(node_lhs[...], node_hot[...])
        contact = contact[: 3 * rows] + contact[3 * rows :]
        for k in range(3):
            fresh = velocity_rows(k) + TIME_STEP * (
                internal[k] + contact[k * rows : (k + 1) * rows]
            ) / mass
            vel[pl.ds(k * 2 * rows, rows), :] = fresh
            pos[pl.ds(k * rows, rows), :] = pos[pl.ds(k * rows, rows), :] + TIME_STEP * fresh
        if step + 1 < STEPS:
            fill_slots(step + 1)
            fill_edges(step + 1)

    for i in range(rows):
        cols = pl.ds(i * LANES, LANES)
        coords_out[:, cols] = pos[pl.ds(i, 3, stride=rows), :]
        velocity_out[:, cols] = vel[pl.ds(i, 3, stride=2 * rows), :]
    for copy in prev_copies():
        copy.wait_send()
    for step in range(STEPS):
        for copy in edge_copies(step):
            copy.wait_send()
        for j in range(count):
            group_copy(step, j, False).wait_send()
            group_copy(step, j, True).wait_send()


def put_out(coords_in, velocity_in, stress_in, coords_out, velocity_out, stress_out, sems):
    pairs = ((coords_in, coords_out), (velocity_in, velocity_out), (stress_in, stress_out))
    copies = [pltpu.make_async_copy(src, dst, sems.at[n]) for n, (src, dst) in enumerate(pairs)]
    for copy in copies:
        copy.start()
    for copy in copies:
        copy.wait()


def per_device(
    sizes, coords, velocity, node_mass, corner_nodes, shape_grad, frame_angles, volume, stress,
    send_nodes, tile_count, tile_nodes, tile_facets, pair_mask,
):
    count = coords.shape[1]
    rows = count // LANES
    group = sizes[1] * sizes[2]
    cap = send_nodes.shape[2]
    tiles = tile_nodes.shape[0]
    spans = group * cap // LANES
    vmem = pl.BlockSpec(memory_space=pltpu.VMEM)
    hbm = pl.BlockSpec(memory_space=pltpu.HBM)
    state = jax.ShapeDtypeStruct((3, count), F32)
    halves = cap // LANES
    arrays = (
        coords, velocity, node_mass.reshape(rows, LANES), corner_nodes, shape_grad, frame_angles,
        volume.reshape(rows, LANES), stress, send_nodes, tile_nodes, tile_facets, pair_mask,
    )
    arrays = tuple(pltpu.with_memory_space_constraint(a, pltpu.HBM) for a in arrays)
    dma = pltpu.SemaphoreType.DMA
    finals = pl.pallas_call(
        functools.partial(kernel, sizes),
        out_shape=(state, state, state),
        in_specs=[hbm] * 12 + [pl.BlockSpec(memory_space=pltpu.SMEM)],
        out_specs=(vmem, vmem, vmem),
        scratch_shapes=[pltpu.VMEM(a.shape, a.dtype) for a in arrays] + [
            dma((len(arrays),)),
            pltpu.VMEM((3 * rows, LANES), F32),
            pltpu.VMEM((6 * rows, LANES), F32),
            pltpu.VMEM((4 * rows, LANES), jnp.int32),
            pltpu.VMEM((8 * rows, LANES), F32),
            pltpu.VMEM((3 * rows, LANES), F32),
            pltpu.VMEM((2 * rows, LANES), F32),
            pltpu.VMEM((group, halves, LANES), jnp.int32),
            pltpu.VMEM((-(-5 * tiles // 8) * 8, LANES), jnp.int32),
            pltpu.VMEM((rows + 1, LANES, 4 * LANES), BF16),
            pltpu.VMEM((LANES, 5 * tiles * LANES), BF16),
            pltpu.VMEM((LANES, group * cap), BF16),
            pltpu.VMEM((4, 16 * (rows + 1), LANES), F32),
            pltpu.VMEM((8 * (rows + 1), LANES), F32),
            pltpu.VMEM((6 * spans, 5 * tiles * LANES), BF16),
            pltpu.VMEM((6 * rows, group * cap), BF16),
            pltpu.VMEM((group, 6 * halves, LANES), F32),
            pltpu.VMEM((group, 6 * halves, LANES), F32),
            pltpu.VMEM((STEPS - 1, group, 3 * halves, LANES), F32),
            pltpu.VMEM((STEPS - 1, group, 3 * halves, LANES), F32),
            pltpu.VMEM((STEPS, group, 3 * halves, LANES), F32),
            pltpu.VMEM((STEPS, group, 3 * halves, LANES), F32),
            pltpu.VMEM((STEPS - 1, 3, LANES), F32),
            pltpu.VMEM((STEPS - 1, 3, LANES), F32),
            pltpu.VMEM((STEPS, 3, LANES), F32),
            pltpu.VMEM((STEPS, 3, LANES), F32),
            pltpu.VMEM((4, LANES), jnp.int32),
            pltpu.VMEM((8, LANES), F32),
            pltpu.VMEM((2, LANES), F32),
            pltpu.VMEM((1, LANES), F32),
            pltpu.VMEM((3, LANES), F32),
            dma((STEPS, group - 1)),
            dma((STEPS, group)),
            dma((STEPS, group - 1)),
            dma((STEPS, group)),
            dma((STEPS, 2)),
            dma((STEPS, 2)),
            dma((5,)),
            dma((5,)),
        ],
        compiler_params=pltpu.CompilerParams(
            collective_id=0, has_side_effects=True, vmem_limit_bytes=24 * 1024 * 1024
        ),
    )(*arrays, tile_count)
    return pl.pallas_call(
        put_out,
        out_shape=(state, state, state),
        in_specs=[vmem] * 3,
        out_specs=(hbm, hbm, hbm),
        scratch_shapes=[dma((3,))],
        compiler_params=pltpu.CompilerParams(vmem_limit_bytes=1024 * 1024),
    )(*finals)


def solution(mesh):
    axes = ("len", "wid", "dep")
    flat, wide = P(axes), P(None, axes)
    sizes = tuple(mesh.shape[name] for name in axes)
    return jax.shard_map(
        functools.partial(per_device, sizes),
        mesh=mesh,
        in_specs=(
            wide, wide, flat, wide, wide, wide, flat, wide,
            P(axes, None, None), flat, P(axes, None), P(None, axes, None), P(axes, None, None),
        ),
        out_specs=(wide, wide, wide),
        check_vma=False,
    )
```

time: 35.4 us -> 31.8 us (0.90)
  Pallas kernels: 33.8 us -> 30.2 us
    pallas_call x2, Pallas kernels: 33.8 us -> 30.2 us  [the longest x1 29.6 us: per_device(): pl.pallas_call(functools.partial(kernel, sizes), out_shape=(state, state,...]
where the time goes in v1:
time: 31.8 us; the launch traced here: 31.5 us
  Pallas kernels  30.2 us (95%)
  between operations  1.29 us (4%)
    pallas_call x1, Pallas kernels, per_device(): pl.pallas_call(functools.partial(kernel, sizes), out_shape=(state, state,...  29.6 us
    pallas_call x1, Pallas kernels, per_device(): pl.pallas_call(put_out, out_shape=(state, state, state), in_specs=[vmem]...  0.65 us

profile of v1, /device:TPU:0, one launch (start us, length us, event | category | flops | bytes accessed | tf_op | source)
XLA Modules:
  0.0 31.5 jit_solution(6525409975532267800)
XLA Ops:
  1.3 29.6 %shard_map.148 = (f32[3,1024]{1,0:T(4,128)S(1)}, f32[3,1024]{1,0:T(4,128)S(1)}, f32[3,1024]{1,0:T(4,128)S(1)}) custom-call(f32[3,1024]{1,0:T(4,128)} %coords_hbm.1, f32[3,1024]{1,0:T(4,128)} %velocity_hbm.1, f32[8,128]{1,0:T(8,128)} %bitcast.2, s32[4,1024]{1,0:T(4,128)} %corner_hbm.1, f32[8,1024]{1,0:T(8,128)} %grad_hbm.1, f32[2,1024]{1,0:T(2,128)} %angles_hbm.1, ...), custom_call_target="tpu_custom_call" | custom-call | tf_op jit(solution)/shard_map/pallas_call | solution.py:506
  30.9 0.6 %shard_map.149 = (f32[3,1024]{1,0:T(4,128)}, f32[3,1024]{1,0:T(4,128)}, f32[3,1024]{1,0:T(4,128)}) custom-call(f32[3,1024]{1,0:T(4,128)S(1)} %get-tuple-element.6.coords_in, f32[3,1024]{1,0:T(4,128)S(1)} %get-tuple-element.7.velocity_in, f32[3,1024]{1,0:T(4,128)S(1)} %get-tuple-element.8.stress_in), custom_call_target="tpu_custom_call" | custom-call | tf_op jit(solution)/shard_map/pallas_call | solution.py:556

commit v2 on v1

--- a/solution.py
+++ b/solution.py
@@ -46,8 +46,8 @@
     coords_out, velocity_out, stress_out,
     coords_in, velocity_in, mass_in, corner_in, grad_in, angles_in, volume_in, stress_in,
     send_in, nodes_in, facets_in, mask_in, in_sem,
-    pos, vel, corner, grad, stress, angle, slot_ids, tile_ids, win_hot, tile_hot, node_hot,
-    win_rows, force_rows, tile_lhs, node_lhs,
+    pos, vel, corner, grad, stress, angle, slot_ids, tile_ids, win_hot, look_hot, slot_hot, node_hot,
+    win_rows, force_rows, tile_lhs, pairs, column_buf,
     send_buf, recv_buf, again_buf, fresh_buf, back_buf, answer_buf,
     first_buf, last_buf, ghost_recv, last_recv,
     corner_prev, grad_prev, angles_prev, volume_prev, stress_prev,
@@ -58,7 +58,8 @@
     group = n_wid * n_dep
     devices = n_len * group
     rows = coords_in.shape[1] // LANES
-    halves = send_in.shape[2] // LANES
+    cap = send_in.shape[2]
+    halves = cap // LANES
     tiles = nodes_in.shape[0]
     my_len = lax.axis_index("len")
     my_wid = lax.axis_index("wid")
@@ -121,24 +122,26 @@
             first_buf[step - 1, pl.ds(k, 1), :] = vel[pl.ds(k * 2 * rows, 1), :]
             last_buf[step - 1, pl.ds(k, 1), :] = vel[pl.ds(k * 2 * rows + rows - 1, 1), :]
 
-    def fill_slots(step):
+    segment = group // 2
+    bases = [pl.multiple_of(side * segment, segment) for side in (1 - upper, upper)]
+
+    def fill_slots(step, base):
         tables = [velocity_rows(k) for k in range(3)]
         if step == 0:
             tables += [pos[pl.ds(k * rows, rows), :] for k in range(3)]
+        target = send_buf if step == 0 else again_buf.at[step - 1]
         for half in range(halves):
-            ids = send_in[0, :, pl.ds(half * LANES, LANES)]
+            cols = pl.ds(half * LANES, LANES)
+            ids = send_in[0, pl.ds(base, segment), cols]
             low, high = ids & (LANES - 1), ids >> 7
             if step == 0:
-                slot_ids[:, half, :] = ids
+                slot_ids[pl.ds(base, segment), half, :] = high
             for c, table in enumerate(tables):
                 found = jnp.zeros(ids.shape, F32)
                 for h in range(rows):
                     row = jnp.broadcast_to(table[h : h + 1], ids.shape)
                     found = jnp.where(high == h, lane_take(row, low), found)
-                if step == 0:
-                    send_buf[:, c * halves + half, :] = found
-                else:
-                    again_buf[step - 1, :, c * halves + half, :] = found
+                target[pl.ds(base, segment), c, cols] = found
 
     def remote(src, dst, send_sem, recv_sem, target):
         return pltpu.make_async_remote_copy(
@@ -169,39 +172,48 @@
             for n, (src, dst) in enumerate(pairs)
         ]
 
-    def group_copy(step, j, back):
+    def ends(step, back):
+        if back:
+            return back_buf.at[step], answer_buf.at[step], back_send_sem, back_recv_sem, 3
+        if step == 0:
+            return send_buf, recv_buf, out_send_sem, out_recv_sem, 6
+        return again_buf.at[step - 1], fresh_buf.at[step - 1], out_send_sem, out_recv_sem, 3
+
+    def group_copy(step, j, back, arriving=False):
         wid, dep = peers[j]
-        place = places[j]
-        if back:
-            src, dst, ss, rs = back_buf.at[step], answer_buf.at[step], back_send_sem, back_recv_sem
-        elif step == 0:
-            src, dst, ss, rs = send_buf, recv_buf, out_send_sem, out_recv_sem
-        else:
-            src, dst, ss, rs = again_buf.at[step - 1], fresh_buf.at[step - 1], out_send_sem, out_recv_sem
+        src, dst, ss, rs, depth = ends(step, back)
+        slot = places[j] if arriving else my_place
         return remote(
-            src.at[place], dst.at[my_place], ss.at[step, j], rs.at[step, my_place], (my_len, wid, dep)
+            src.at[places[j], pl.ds(0, depth)], dst.at[slot, pl.ds(0, depth)],
+            ss.at[step, j], rs.at[step, slot], (my_len, wid, dep),
         )
 
-    def group_arrival(step, j, back):
-        wid, dep = peers[j]
-        place = places[j]
-        if back:
-            src, dst, ss, rs = back_buf.at[step], answer_buf.at[step], back_send_sem, back_recv_sem
-        elif step == 0:
-            src, dst, ss, rs = send_buf, recv_buf, out_send_sem, out_recv_sem
-        else:
-            src, dst, ss, rs = again_buf.at[step - 1], fresh_buf.at[step - 1], out_send_sem, out_recv_sem
-        return remote(
-            src.at[place], dst.at[place], ss.at[step, j], rs.at[step, place], (my_len, wid, dep)
-        )
-
-    fill_slots(0)
+    batch = group // 2
+    far_count = n_dep * (n_wid // 2)
+    parts = ((bases[0], range(far_count)), (bases[1], range(far_count, count)))
+
+    fill_slots(0, bases[0])
     pl.semaphore_wait(barrier, group + 1)
 
     sub = lax.broadcasted_iota(jnp.int32, (LANES, LANES), 0)
+    lane = lax.broadcasted_iota(jnp.int32, (LANES, LANES), 1)
+    lane_tall = lax.broadcasted_iota(jnp.int32, (cap, LANES), 1)
+    eight = lax.broadcasted_iota(jnp.int32, (8, LANES), 0)
+    row_iota = lax.broadcasted_iota(jnp.int32, (rows, LANES), 0)
+    group_iota = lax.broadcasted_iota(jnp.int32, (group, LANES), 0)
+
+    def split(values):
+        first = values.astype(BF16).astype(F32)
+        return first, values - first
+
     for step in range(STEPS):
-        for j in range(count):
-            group_copy(step, j, False).start()
+        for base, span in parts:
+            if step or base is not bases[0]:
+                fill_slots(step, base)
+            for j in span:
+                group_copy(step, j, False).start()
+        if step:
+            fill_edges(step)
         for copy in edge_copies(step):
             copy.start()
 
@@ -240,59 +252,70 @@
             gx = [grad[pl.ds(a * rows, rows), :] for a in range(4)]
             gy = [grad[pl.ds((4 + a) * rows, rows), :] for a in range(4)]
             own = (frame(polar, azim), volume, gx, gy, corner_low, corner_far)
+            slots_high = tile_ids[...] // cap
+            slots_low = tile_ids[...] % cap
+            low_columns = jnp.transpose(slots_low)
+            node_columns = jnp.transpose(send_in[0] & (LANES - 1))
+            for g in range(group):
+                column_buf[pl.ds(g * cap, cap), :] = jnp.broadcast_to(node_columns[:, g : g + 1], (cap, LANES))
             for b in range(5 * tiles):
-                low = tile_ids[pl.ds(b, 1), :] & (LANES - 1)
-                tile_hot[:, pl.ds(b * LANES, LANES)] = (sub == low).astype(F32).astype(BF16)
+                cols = pl.ds(b * LANES, LANES)
+                for half in range(halves):
+                    span = pl.ds(half * LANES, LANES)
+                    hot = sub + half * LANES == slots_low[b : b + 1]
+                    look_hot[span, cols] = hot.astype(F32).astype(BF16)
+                    hot = lane + half * LANES == low_columns[:, b : b + 1]
+                    slot_hot[cols, span] = hot.astype(F32).astype(BF16)
             for n, g in enumerate(arrival):
-                for half in range(halves):
-                    low = slot_ids[g, pl.ds(half, 1), :] & (LANES - 1)
-                    node_hot[:, pl.ds((n * halves + half) * LANES, LANES)] = (
-                        (sub == low).astype(F32).astype(BF16)
-                    )
-            ids = tile_ids[...]
-            ids_low, ids_high = ids & (LANES - 1), ids >> 7
-
-        mine = send_buf if step == 0 else again_buf.at[step - 1]
-        landed = recv_buf if step == 0 else fresh_buf.at[step - 1]
-        found = [jnp.zeros(ids.shape, F32) for c in range(6 if step == 0 else 3)]
-        for n, g in enumerate(arrival):
-            if n:
-                group_arrival(step, count - n, False).wait_recv()
-            source = landed if n else mine
-            for half in range(halves):
-                match = ids_high == g * halves + half
-                for c in range(len(found)):
-                    row = jnp.broadcast_to(source[g, pl.ds(c * halves + half, 1), :], ids.shape)
-                    found[c] = jnp.where(match, lane_take(row, ids_low), found[c])
-        if step == 0:
-            slot_pos = found[3:]
-        else:
-            slot_pos = [slot_pos[k] + TIME_STEP * found[k] for k in range(3)]
-        state = slot_pos + found[:3]
-        centre = [
-            0.25 * sum(s[(a + 1) * tiles : (a + 2) * tiles] for a in range(4)) for s in state
+                hot = lane_tall == column_buf[pl.ds(pl.multiple_of(g * cap, cap), cap), :]
+                node_hot[pl.ds(n * cap, cap), :] = hot.astype(F32).astype(BF16)
+
+        mine, landed = (send_buf, recv_buf) if step == 0 else (again_buf.at[step - 1], fresh_buf.at[step - 1])
+        landed[my_place] = mine[my_place]
+        for j in range(count)[::-1]:
+            group_copy(step, j, False, True).wait_recv()
+        table = []
+        for g in range(group):
+            table += [part.astype(BF16) for part in split(landed[g])]
+        table = jnp.concatenate(table, axis=0)
+        state = []
+        for b in range(0, 5 * tiles, 2):
+            looked = nn_dot(table, look_hot[:, pl.ds(b * LANES, 2 * LANES)])
+            for side in range(2):
+                high = jnp.broadcast_to(slots_high[b + side : b + side + 1], (8, LANES))
+                block = looked[:, side * LANES : (side + 1) * LANES]
+                first, second = block[:8], block[8:16]
+                for g in range(1, group):
+                    match = high == g
+                    first = jnp.where(match, block[g * 16 : g * 16 + 8], first)
+                    second = jnp.where(match, block[g * 16 + 8 : g * 16 + 16], second)
+                state.append(first + second)
+        bodies = state[:tiles] + [
+            0.25 * sum(state[(a + 1) * tiles + t] for a in range(4)) for t in range(tiles)
         ]
-        nodes = [s[:tiles] for s in state]
-        node_mix = [STIFFNESS * nodes[k] - DAMPING * nodes[3 + k] for k in range(3)]
-        facet_mix = [STIFFNESS * centre[k] - DAMPING * centre[3 + k] for k in range(3)]
-        lead = jnp.concatenate(nodes[:3] + [jnp.zeros((16 - 3 * tiles % 16, LANES), F32)], axis=0)
-        columns = jnp.transpose(lead)
-        ones = jnp.ones((1, LANES), F32)
-        blank = jnp.zeros((4, LANES), F32)
-        node_force = [[None] * tiles for k in range(3)]
-        facet_force = [[None] * tiles for k in range(3)]
+        if step:
+            bodies = [
+                jnp.where(eight < 3, new, old + TIME_STEP * jnp.roll(new, 3, axis=0))
+                for new, old in zip(bodies, old_bodies)
+            ]
+        old_bodies = bodies
+        mixes = [
+            jnp.where(eight < 3, STIFFNESS * jnp.roll(body, 5, axis=0) - DAMPING * body, 0.0)
+            for body in bodies
+        ]
+        sides = [jnp.where(eight == 3, 1.0, mix) for mix in mixes]
+        columns = jnp.transpose(jnp.concatenate(bodies[:tiles], axis=0))
+        forces = []
         for t in range(tiles):
             live = jnp.where(t < count_in[0], 1.0, 0.0)
             dist = jnp.zeros((LANES, LANES), F32)
-            for k in range(3):
-                gap = columns[:, k * tiles + t : k * tiles + t + 1] - centre[k][t : t + 1]
+            for k in range(3, 6):
+                gap = columns[:, 8 * t + k : 8 * t + k + 1] - bodies[tiles + t][k : k + 1]
                 dist += gap * gap
             weight = mask_in[t].astype(F32) * (live * jnp.maximum(RADIUS_SQ - dist, 0.0))
             w1, w2 = two_parts(weight)
-            a1, a2 = two_parts(jnp.concatenate([m[t : t + 1] for m in node_mix] + [ones, blank], axis=0))
-            b1, b2 = two_parts(jnp.concatenate([m[t : t + 1] for m in facet_mix] + [ones, blank], axis=0))
-            left_a = jnp.concatenate([a1, a2], axis=0)
-            left_b = jnp.concatenate([b1, b2], axis=0)
+            left_a = jnp.concatenate(two_parts(sides[t]), axis=0)
+            left_b = jnp.concatenate(two_parts(sides[tiles + t]), axis=0)
             to_facet = nn_dot(
                 jnp.concatenate([left_a, left_a], axis=1), jnp.concatenate([w1, w2], axis=0)
             )
@@ -301,27 +324,21 @@
             )
             to_facet = to_facet[:8] + to_facet[8:]
             to_node = to_node[:8] + to_node[8:]
-            for k in range(3):
-                node_force[k][t] = node_mix[k][t : t + 1] * to_node[3:4] - to_node[k : k + 1]
-                facet_force[k][t] = -0.25 * (
-                    to_facet[k : k + 1] - to_facet[3:4] * facet_mix[k][t : t + 1]
-                )
-        spans = halves * group
-        high_iota = lax.broadcasted_iota(jnp.int32, (spans, LANES), 0)
-        for b in range(5 * tiles):
-            high = ids_high[b : b + 1]
-            match = high_iota == (high % halves) * group + high // halves
-            for k in range(3):
-                row = node_force[k][b] if b < tiles else facet_force[k][b % tiles]
-                chosen = jnp.where(match, jnp.broadcast_to(row, match.shape), 0.0)
-                p1, p2 = two_parts(chosen)
-                cols = pl.ds(b * LANES, LANES)
-                tile_lhs[pl.ds(k * spans, spans), cols] = p1
-                tile_lhs[pl.ds((3 + k) * spans, spans), cols] = p2
-        slots = nt_dot(tile_lhs[...], tile_hot[...])
-        slots = slots[: 3 * spans] + slots[3 * spans :]
-        for r in range(3 * halves):
-            back_buf[step, :, r, :] = slots[r * group : (r + 1) * group]
+            node_force = mixes[t] * to_node[3:4] - to_node
+            facet_force = -0.25 * (to_facet - to_facet[3:4] * mixes[tiles + t])
+            for force, blocks in ((node_force, [t]), (facet_force, [(a + 1) * tiles + t for a in range(4)])):
+                matches = [group_iota == slots_high[b : b + 1] for b in blocks]
+                for part, value in enumerate(split(force)):
+                    for k in range(3):
+                        row = jnp.broadcast_to(value[k : k + 1], (group, LANES))
+                        for b, match in zip(blocks, matches):
+                            tile_lhs[pl.ds((part * 3 + k) * group, group), pl.ds(b * LANES, LANES)] = (
+                                jnp.where(match, row, 0.0).astype(BF16)
+                            )
+        slots = nn_dot(tile_lhs[...], slot_hot[...])
+        slots = slots[: 3 * group] + slots[3 * group :]
+        for k in range(3):
+            back_buf[step, :, k, :] = slots[k * group : (k + 1) * group]
         for j in range(count):
             group_copy(step, j, True).start()
 
@@ -429,36 +446,31 @@
             for k in range(3):
                 for i in range(rows):
                     stress_out[pl.ds(k, 1), pl.ds(i * LANES, LANES)] = own_stress[k][i : i + 1]
-        row_iota = lax.broadcasted_iota(jnp.int32, (rows, LANES), 0)
-        for n, g in enumerate(arrival):
-            if n:
-                group_arrival(step, count - n, True).wait_recv()
-            source = answer_buf if n else back_buf
-            for half in range(halves):
-                high = slot_ids[g, pl.ds(half, 1), :] >> 7
-                match = row_iota == high
-                chosen = jnp.concatenate([
-                    jnp.where(
-                        match,
-                        jnp.broadcast_to(source[step, g, pl.ds(k * halves + half, 1), :], match.shape),
-                        0.0,
-                    )
-                    for k in range(3)
-                ], axis=0)
-                first = chosen.astype(BF16).astype(F32)
-                both = jnp.concatenate([first, chosen - first], axis=0).astype(BF16)
-                node_lhs[:, pl.ds((n * halves + half) * LANES, LANES)] = both
-        contact = nt_dot(node_lhs[...], node_hot[...])
-        contact = contact[: 3 * rows] + contact[3 * rows :]
+        contact = jnp.zeros((3 * rows, LANES), F32)
+        for begin in range(0, group, batch):
+            for n in range(max(begin, 1), begin + batch):
+                group_copy(step, count - n, True, True).wait_recv()
+            for n in range(begin, begin + batch):
+                g = arrival[n]
+                source = answer_buf if n else back_buf
+                halved = split(source[step, g])
+                for half in range(halves):
+                    match = row_iota == slot_ids[g, pl.ds(half, 1), :]
+                    at = pl.ds((n * halves + half) * LANES, LANES)
+                    for part in range(2):
+                        for k in range(3):
+                            row = halved[part][k : k + 1, half * LANES : (half + 1) * LANES]
+                            chosen = jnp.where(match, jnp.broadcast_to(row, match.shape), 0.0)
+                            pairs[pl.ds((part * 3 + k) * rows, rows), at] = chosen.astype(BF16)
+            at = pl.ds(begin * cap, batch * cap)
+            summed = nn_dot(pairs[:, at], node_hot[at, :])
+            contact += summed[: 3 * rows] + summed[3 * rows :]
         for k in range(3):
             fresh = velocity_rows(k) + TIME_STEP * (
                 internal[k] + contact[k * rows : (k + 1) * rows]
             ) / mass
             vel[pl.ds(k * 2 * rows, rows), :] = fresh
             pos[pl.ds(k * rows, rows), :] = pos[pl.ds(k * rows, rows), :] + TIME_STEP * fresh
-        if step + 1 < STEPS:
-            fill_slots(step + 1)
-            fill_edges(step + 1)
 
     for i in range(rows):
         cols = pl.ds(i * LANES, LANES)
@@ -492,7 +504,6 @@
     group = sizes[1] * sizes[2]
     cap = send_nodes.shape[2]
     tiles = tile_nodes.shape[0]
-    spans = group * cap // LANES
     vmem = pl.BlockSpec(memory_space=pltpu.VMEM)
     hbm = pl.BlockSpec(memory_space=pltpu.HBM)
     state = jax.ShapeDtypeStruct((3, count), F32)
@@ -519,18 +530,20 @@
             pltpu.VMEM((group, halves, LANES), jnp.int32),
             pltpu.VMEM((-(-5 * tiles // 8) * 8, LANES), jnp.int32),
             pltpu.VMEM((rows + 1, LANES, 4 * LANES), BF16),
-            pltpu.VMEM((LANES, 5 * tiles * LANES), BF16),
-            pltpu.VMEM((LANES, group * cap), BF16),
+            pltpu.VMEM((cap, 5 * tiles * LANES), BF16),
+            pltpu.VMEM((5 * tiles * LANES, cap), BF16),
+            pltpu.VMEM((group * cap, LANES), BF16),
             pltpu.VMEM((4, 16 * (rows + 1), LANES), F32),
             pltpu.VMEM((8 * (rows + 1), LANES), F32),
-            pltpu.VMEM((6 * spans, 5 * tiles * LANES), BF16),
+            pltpu.VMEM((6 * group, 5 * tiles * LANES), BF16),
             pltpu.VMEM((6 * rows, group * cap), BF16),
-            pltpu.VMEM((group, 6 * halves, LANES), F32),
-            pltpu.VMEM((group, 6 * halves, LANES), F32),
-            pltpu.VMEM((STEPS - 1, group, 3 * halves, LANES), F32),
-            pltpu.VMEM((STEPS - 1, group, 3 * halves, LANES), F32),
-            pltpu.VMEM((STEPS, group, 3 * halves, LANES), F32),
-            pltpu.VMEM((STEPS, group, 3 * halves, LANES), F32),
+            pltpu.VMEM((group * cap, LANES), jnp.int32),
+            pltpu.VMEM((group, 8, cap), F32),
+            pltpu.VMEM((group, 8, cap), F32),
+            pltpu.VMEM((STEPS - 1, group, 8, cap), F32),
+            pltpu.VMEM((STEPS - 1, group, 8, cap), F32),
+            pltpu.VMEM((STEPS, group, 4, cap), F32),
+            pltpu.VMEM((STEPS, group, 4, cap), F32),
             pltpu.VMEM((STEPS - 1, 3, LANES), F32),
             pltpu.VMEM((STEPS - 1, 3, LANES), F32),
             pltpu.VMEM((STEPS, 3, LANES), F32),

time: 31.8 us -> 29.6 us (0.931)
  Pallas kernels: 30.2 us -> 28 us
    pallas_call x1, Pallas kernels: 29.6 us -> 27.4 us  [per_device(): pl.pallas_call(functools.partial(kernel, sizes), out_shape=(state, state,...]
where the time goes in v2:
time: 29.6 us; the launch traced here: 29.3 us
  Pallas kernels  28 us (95%)
  between operations  1.29 us (4%)
    pallas_call x1, Pallas kernels, per_device(): pl.pallas_call(functools.partial(kernel, sizes), out_shape=(state, state,...  27.4 us
    pallas_call x1, Pallas kernels, per_device(): pl.pallas_call(put_out, out_shape=(state, state, state), in_specs=[vmem]...  0.65 us

profile of v2, /device:TPU:0, one launch (start us, length us, event | category | flops | bytes accessed | tf_op | source)
XLA Modules:
  0.0 29.3 jit_solution(975447271655650050)
XLA Ops:
  1.3 27.4 %shard_map.148 = (f32[3,1024]{1,0:T(4,128)S(1)}, f32[3,1024]{1,0:T(4,128)S(1)}, f32[3,1024]{1,0:T(4,128)S(1)}) custom-call(f32[3,1024]{1,0:T(4,128)} %coords_hbm.1, f32[3,1024]{1,0:T(4,128)} %velocity_hbm.1, f32[8,128]{1,0:T(8,128)} %bitcast.2, s32[4,1024]{1,0:T(4,128)} %corner_hbm.1, f32[8,1024]{1,0:T(8,128)} %grad_hbm.1, f32[2,1024]{1,0:T(2,128)} %angles_hbm.1, ...), custom_call_target="tpu_custom_call" | custom-call | tf_op jit(solution)/shard_map/pallas_call | solution.py:517
  28.7 0.6 %shard_map.149 = (f32[3,1024]{1,0:T(4,128)}, f32[3,1024]{1,0:T(4,128)}, f32[3,1024]{1,0:T(4,128)}) custom-call(f32[3,1024]{1,0:T(4,128)S(1)} %get-tuple-element.6.coords_in, f32[3,1024]{1,0:T(4,128)S(1)} %get-tuple-element.7.velocity_in, f32[3,1024]{1,0:T(4,128)S(1)} %get-tuple-element.8.stress_in), custom_call_target="tpu_custom_call" | custom-call | tf_op jit(solution)/shard_map/pallas_call | solution.py:569

commit v3 on v2

--- a/solution.py
+++ b/solution.py
@@ -20,6 +20,7 @@
 MESH = pl.DeviceIdType.MESH
 F32 = jnp.float32
 BF16 = jnp.bfloat16
+F8 = jnp.float8_e4m3fn
 
 
 def two_parts(values):
@@ -47,12 +48,11 @@
     coords_in, velocity_in, mass_in, corner_in, grad_in, angles_in, volume_in, stress_in,
     send_in, nodes_in, facets_in, mask_in, in_sem,
     pos, vel, corner, grad, stress, angle, slot_ids, tile_ids, win_hot, look_hot, slot_hot, node_hot,
-    win_rows, force_rows, tile_lhs, pairs, column_buf,
+    win_rows, force_rows, tile_lhs, pairs, column_buf, weight_in,
     send_buf, recv_buf, again_buf, fresh_buf, back_buf, answer_buf,
-    first_buf, last_buf, ghost_recv, last_recv,
+    first_buf, last_buf, edge_recv,
     corner_prev, grad_prev, angles_prev, volume_prev, stress_prev,
-    out_send_sem, out_recv_sem, back_send_sem, back_recv_sem, edge_send_sem, edge_recv_sem,
-    prev_send_sem, prev_recv_sem,
+    send_sem, out_sem, back_sem, edge_sem, prev_sem,
 ):
     n_len, n_wid, n_dep = sizes
     group = n_wid * n_dep
@@ -97,14 +97,12 @@
             (nodes_hbm, nodes_in), (facets_hbm, facets_in), (mask_hbm, mask_in),
         ))
     ]
-    for load in loads[:3]:
-        load.start()
     barrier = pltpu.get_barrier_semaphore()
     for wid, dep in peers:
         pl.semaphore_signal(barrier, inc=1, device_id=(my_len, wid, dep), device_id_type=MESH)
     pl.semaphore_signal(barrier, inc=1, device_id=before, device_id_type=MESH)
     pl.semaphore_signal(barrier, inc=1, device_id=after, device_id_type=MESH)
-    for load in loads[3:]:
+    for load in loads:
         load.start()
     for load in loads[:3]:
         load.wait()
@@ -143,11 +141,14 @@
                     found = jnp.where(high == h, lane_take(row, low), found)
                 target[pl.ds(base, segment), c, cols] = found
 
-    def remote(src, dst, send_sem, recv_sem, target):
+    def remote(src, dst, recv_sem, target):
         return pltpu.make_async_remote_copy(
-            src_ref=src, dst_ref=dst, send_sem=send_sem, recv_sem=recv_sem,
+            src_ref=src, dst_ref=dst, send_sem=send_sem.at[0], recv_sem=recv_sem,
             device_id=target, device_id_type=MESH,
         )
+
+    def drain(ref, sem):
+        pltpu.make_async_copy(ref, ref, sem).wait()
 
     final = pl.ds((rows - 1) * LANES, LANES)
 
@@ -157,8 +158,8 @@
         else:
             first, last = first_buf.at[step - 1], last_buf.at[step - 1]
         return (
-            remote(first, ghost_recv.at[step], edge_send_sem.at[step, 0], edge_recv_sem.at[step, 0], before),
-            remote(last, last_recv.at[step], edge_send_sem.at[step, 1], edge_recv_sem.at[step, 1], after),
+            remote(first, edge_recv.at[step, 0], edge_sem.at[step], before),
+            remote(last, edge_recv.at[step, 1], edge_sem.at[step], after),
         )
 
     def prev_copies():
@@ -168,28 +169,24 @@
             (volume_in.at[pl.ds(rows - 1, 1), :], volume_prev),
         )
         return [
-            remote(src, dst, prev_send_sem.at[n], prev_recv_sem.at[n], after)
-            for n, (src, dst) in enumerate(pairs)
+            remote(src, dst, prev_sem.at[0], after) for src, dst in pairs
         ]
 
-    def ends(step, back):
+    far_count = n_dep * (n_wid // 2)
+
+    def group_copy(step, j, back):
+        wid, dep = peers[j]
         if back:
-            return back_buf.at[step], answer_buf.at[step], back_send_sem, back_recv_sem, 3
-        if step == 0:
-            return send_buf, recv_buf, out_send_sem, out_recv_sem, 6
-        return again_buf.at[step - 1], fresh_buf.at[step - 1], out_send_sem, out_recv_sem, 3
-
-    def group_copy(step, j, back, arriving=False):
-        wid, dep = peers[j]
-        src, dst, ss, rs, depth = ends(step, back)
-        slot = places[j] if arriving else my_place
+            src, dst, depth, sem = back_buf.at[step], answer_buf.at[step], 3, back_sem.at[step, int(j < far_count)]
+        elif step == 0:
+            src, dst, depth, sem = send_buf, recv_buf, 6, out_sem.at[step]
+        else:
+            src, dst, depth, sem = again_buf.at[step - 1], fresh_buf.at[step - 1], 3, out_sem.at[step]
         return remote(
-            src.at[places[j], pl.ds(0, depth)], dst.at[slot, pl.ds(0, depth)],
-            ss.at[step, j], rs.at[step, slot], (my_len, wid, dep),
+            src.at[places[j], pl.ds(0, depth)], dst.at[my_place, pl.ds(0, depth)], sem, (my_len, wid, dep)
         )
 
-    batch = group // 2
-    far_count = n_dep * (n_wid // 2)
+    batch = count + 1 - far_count
     parts = ((bases[0], range(far_count)), (bases[1], range(far_count, count)))
 
     fill_slots(0, bases[0])
@@ -200,6 +197,7 @@
     lane_tall = lax.broadcasted_iota(jnp.int32, (cap, LANES), 1)
     eight = lax.broadcasted_iota(jnp.int32, (8, LANES), 0)
     row_iota = lax.broadcasted_iota(jnp.int32, (rows, LANES), 0)
+    eight_wide = lax.broadcasted_iota(jnp.int32, (8, cap), 0)
     group_iota = lax.broadcasted_iota(jnp.int32, (group, LANES), 0)
 
     def split(values):
@@ -229,9 +227,13 @@
                 grad[pl.ds(i, 8, stride=rows), :] = grad_in[:, cols]
                 angle[pl.ds(i, 2, stride=rows), :] = angles_in[:, cols]
             tile_ids[...] = jnp.zeros_like(tile_ids)
-            tile_ids[pl.ds(0, tiles), :] = nodes_in[...]
-            for a in range(4):
-                tile_ids[pl.ds((a + 1) * tiles, tiles), :] = facets_in[a]
+            for t in range(tiles):
+                tile_ids[pl.ds(5 * t, 1), :] = nodes_in[pl.ds(t, 1), :]
+                for a in range(4):
+                    tile_ids[pl.ds(5 * t + 1 + a, 1), :] = facets_in[a, pl.ds(t, 1), :]
+                live = jnp.where(t < count_in[0], 1.0, 0.0)
+                weight_in[t] = mask_in[t].astype(F32) * live
+            old_bodies = {}
             first_row = lax.broadcasted_iota(jnp.int32, (rows, LANES), 0) * LANES
             corner_low, corner_far = [], []
             for a in range(4):
@@ -263,79 +265,90 @@
                 for half in range(halves):
                     span = pl.ds(half * LANES, LANES)
                     hot = sub + half * LANES == slots_low[b : b + 1]
-                    look_hot[span, cols] = hot.astype(F32).astype(BF16)
+                    look_hot[span, cols] = hot.astype(F32).astype(F8)
                     hot = lane + half * LANES == low_columns[:, b : b + 1]
-                    slot_hot[cols, span] = hot.astype(F32).astype(BF16)
+                    slot_hot[cols, span] = hot.astype(F32).astype(F8)
             for n, g in enumerate(arrival):
                 hot = lane_tall == column_buf[pl.ds(pl.multiple_of(g * cap, cap), cap), :]
-                node_hot[pl.ds(n * cap, cap), :] = hot.astype(F32).astype(BF16)
+                node_hot[pl.ds(n * cap, cap), :] = hot.astype(F32).astype(F8)
 
         mine, landed = (send_buf, recv_buf) if step == 0 else (again_buf.at[step - 1], fresh_buf.at[step - 1])
         landed[my_place] = mine[my_place]
-        for j in range(count)[::-1]:
-            group_copy(step, j, False, True).wait_recv()
+        depth = 6 if step == 0 else 3
+        drain(landed.at[pl.ds(0, count), pl.ds(0, depth)], out_sem.at[step])
         table = []
+        deep = 16 if step == 0 else 8
         for g in range(group):
-            table += [part.astype(BF16) for part in split(landed[g])]
-        table = jnp.concatenate(table, axis=0)
+            first, second = split(landed[g])
+            if step == 0:
+                table += [first, second]
+            else:
+                table.append(jnp.where(eight_wide < 4, first, jnp.roll(second, 4, axis=0)))
+        table = jnp.concatenate(table, axis=0).astype(BF16)
         state = []
         for b in range(0, 5 * tiles, 2):
             looked = nn_dot(table, look_hot[:, pl.ds(b * LANES, 2 * LANES)])
             for side in range(2):
                 high = jnp.broadcast_to(slots_high[b + side : b + side + 1], (8, LANES))
                 block = looked[:, side * LANES : (side + 1) * LANES]
-                first, second = block[:8], block[8:16]
+                first, second = block[:8], block[deep - 8 : deep]
                 for g in range(1, group):
                     match = high == g
-                    first = jnp.where(match, block[g * 16 : g * 16 + 8], first)
-                    second = jnp.where(match, block[g * 16 + 8 : g * 16 + 16], second)
-                state.append(first + second)
-        bodies = state[:tiles] + [
-            0.25 * sum(state[(a + 1) * tiles + t] for a in range(4)) for t in range(tiles)
-        ]
-        if step:
-            bodies = [
-                jnp.where(eight < 3, new, old + TIME_STEP * jnp.roll(new, 3, axis=0))
-                for new, old in zip(bodies, old_bodies)
-            ]
-        old_bodies = bodies
-        mixes = [
-            jnp.where(eight < 3, STIFFNESS * jnp.roll(body, 5, axis=0) - DAMPING * body, 0.0)
-            for body in bodies
-        ]
-        sides = [jnp.where(eight == 3, 1.0, mix) for mix in mixes]
-        columns = jnp.transpose(jnp.concatenate(bodies[:tiles], axis=0))
-        forces = []
-        for t in range(tiles):
-            live = jnp.where(t < count_in[0], 1.0, 0.0)
-            dist = jnp.zeros((LANES, LANES), F32)
-            for k in range(3, 6):
-                gap = columns[:, 8 * t + k : 8 * t + k + 1] - bodies[tiles + t][k : k + 1]
-                dist += gap * gap
-            weight = mask_in[t].astype(F32) * (live * jnp.maximum(RADIUS_SQ - dist, 0.0))
-            w1, w2 = two_parts(weight)
-            left_a = jnp.concatenate(two_parts(sides[t]), axis=0)
-            left_b = jnp.concatenate(two_parts(sides[tiles + t]), axis=0)
-            to_facet = nn_dot(
-                jnp.concatenate([left_a, left_a], axis=1), jnp.concatenate([w1, w2], axis=0)
-            )
-            to_node = nt_dot(
-                jnp.concatenate([left_b, left_b], axis=1), jnp.concatenate([w1, w2], axis=1)
-            )
-            to_facet = to_facet[:8] + to_facet[8:]
-            to_node = to_node[:8] + to_node[8:]
-            node_force = mixes[t] * to_node[3:4] - to_node
-            facet_force = -0.25 * (to_facet - to_facet[3:4] * mixes[tiles + t])
-            for force, blocks in ((node_force, [t]), (facet_force, [(a + 1) * tiles + t for a in range(4)])):
-                matches = [group_iota == slots_high[b : b + 1] for b in blocks]
-                for part, value in enumerate(split(force)):
-                    for k in range(3):
-                        row = jnp.broadcast_to(value[k : k + 1], (group, LANES))
-                        for b, match in zip(blocks, matches):
-                            tile_lhs[pl.ds((part * 3 + k) * group, group), pl.ds(b * LANES, LANES)] = (
-                                jnp.where(match, row, 0.0).astype(BF16)
-                            )
-        slots = nn_dot(tile_lhs[...], slot_hot[...])
+                    first = jnp.where(match, block[g * deep : g * deep + 8], first)
+                    if step == 0:
+                        second = jnp.where(match, block[g * deep + 8 : g * deep + 16], second)
+                state.append(first + (second if step == 0 else jnp.roll(first, 4, axis=0)))
+        slots = jnp.zeros((6 * group, cap), F32)
+        for pair in range(tiles // 2):
+            pair_tiles = (2 * pair, 2 * pair + 1)
+            bodies = {}
+            for t in pair_tiles:
+                bodies[t, 0] = state[5 * t]
+                bodies[t, 1] = 0.25 * sum(state[5 * t + 1 + a] for a in range(4))
+            if step:
+                for at in bodies:
+                    moved = old_bodies[at] + TIME_STEP * jnp.roll(bodies[at], 3, axis=0)
+                    bodies[at] = jnp.where(eight < 3, bodies[at], moved)
+            if step + 1 < STEPS:
+                old_bodies.update(bodies)
+            columns = jnp.transpose(jnp.concatenate([bodies[t, 0] for t in pair_tiles], axis=0))
+            for t in pair_tiles:
+                mixes = [
+                    jnp.where(
+                        eight < 3, STIFFNESS * jnp.roll(bodies[t, s], 5, axis=0) - DAMPING * bodies[t, s], 0.0
+                    )
+                    for s in range(2)
+                ]
+                left_a, left_b = [
+                    jnp.concatenate(two_parts(jnp.where(eight == 3, 1.0, mix)), axis=0) for mix in mixes
+                ]
+                dist = jnp.zeros((LANES, LANES), F32)
+                for k in range(3, 6):
+                    at = 8 * (t % 2) + k
+                    gap = columns[:, at : at + 1] - bodies[t, 1][k : k + 1]
+                    dist += gap * gap
+                w1, w2 = two_parts(weight_in[t] * jnp.maximum(RADIUS_SQ - dist, 0.0))
+                to_facet = nn_dot(
+                    jnp.concatenate([left_a, left_a], axis=1), jnp.concatenate([w1, w2], axis=0)
+                )
+                to_node = nt_dot(
+                    jnp.concatenate([left_b, left_b], axis=1), jnp.concatenate([w1, w2], axis=1)
+                )
+                to_facet = to_facet[:8] + to_facet[8:]
+                to_node = to_node[:8] + to_node[8:]
+                node_force = mixes[0] * to_node[3:4] - to_node
+                facet_force = -0.25 * (to_facet - to_facet[3:4] * mixes[1])
+                for force, blocks in ((node_force, [5 * t]), (facet_force, [5 * t + 1 + a for a in range(4)])):
+                    matches = [group_iota == slots_high[b : b + 1] for b in blocks]
+                    for part, value in enumerate(split(force)):
+                        for k in range(3):
+                            row = jnp.broadcast_to(value[k : k + 1], (group, LANES))
+                            for b, match in zip(blocks, matches):
+                                tile_lhs[pl.ds((part * 3 + k) * group, group), pl.ds(b * LANES, LANES)] = (
+                                    jnp.where(match, row, 0.0).astype(BF16)
+                                )
+            at = pl.ds(pair * 10 * LANES, 10 * LANES)
+            slots += nn_dot(tile_lhs[:, at], slot_hot[at, :])
         slots = slots[: 3 * group] + slots[3 * group :]
         for k in range(3):
             back_buf[step, :, k, :] = slots[k * group : (k + 1) * group]
@@ -343,8 +356,7 @@
             group_copy(step, j, True).start()
 
         if step == 0:
-            for copy in prev_copies():
-                copy.wait_recv()
+            drain(force_rows.at[pl.ds(0, 18)], prev_sem.at[0])
 
             def whole(row):
                 return jnp.broadcast_to(row, (8, LANES))
@@ -405,10 +417,9 @@
                 forces.append(parts)
             return [sxx, syy, sxy], forces
 
-        for copy in edge_copies(step):
-            copy.wait_recv()
+        drain(edge_recv.at[step], edge_sem.at[step])
         for k in range(3):
-            vel[pl.ds(k * 2 * rows + rows, 1), :] = ghost_recv[step, pl.ds(k, 1), :]
+            vel[pl.ds(k * 2 * rows + rows, 1), :] = edge_recv[step, 0, pl.ds(k, 1), :]
         own_stress, forces = element_forces(
             own, own_stress,
             [velocity_rows(k) for k in range(3)],
@@ -416,7 +427,7 @@
         )
         prev_stress, prev_forces = element_forces(
             prev, prev_stress,
-            [whole(last_recv[step, pl.ds(k, 1), :]) for k in range(3)],
+            [whole(edge_recv[step, 1, pl.ds(k, 1), :]) for k in range(3)],
             [whole(vel[pl.ds(k * 2 * rows, 1), :]) for k in range(3)],
         )
         for a in range(4):
@@ -446,10 +457,13 @@
             for k in range(3):
                 for i in range(rows):
                     stress_out[pl.ds(k, 1), pl.ds(i * LANES, LANES)] = own_stress[k][i : i + 1]
+        if step + 1 == STEPS:
+            sent = count * halves * (6 + 3 * (STEPS - 1) + 3 * STEPS) + 6 * STEPS + 18
+            drain(column_buf.at[pl.ds(0, sent)], send_sem.at[0])
         contact = jnp.zeros((3 * rows, LANES), F32)
         for begin in range(0, group, batch):
-            for n in range(max(begin, 1), begin + batch):
-                group_copy(step, count - n, True, True).wait_recv()
+            answers = batch - 1 if begin == 0 else batch
+            drain(answer_buf.at[step, pl.ds(0, answers), pl.ds(0, 3)], back_sem.at[step, int(begin > 0)])
             for n in range(begin, begin + batch):
                 g = arrival[n]
                 source = answer_buf if n else back_buf
@@ -476,14 +490,6 @@
         cols = pl.ds(i * LANES, LANES)
         coords_out[:, cols] = pos[pl.ds(i, 3, stride=rows), :]
         velocity_out[:, cols] = vel[pl.ds(i, 3, stride=2 * rows), :]
-    for copy in prev_copies():
-        copy.wait_send()
-    for step in range(STEPS):
-        for copy in edge_copies(step):
-            copy.wait_send()
-        for j in range(count):
-            group_copy(step, j, False).wait_send()
-            group_copy(step, j, True).wait_send()
 
 
 def put_out(coords_in, velocity_in, stress_in, coords_out, velocity_out, stress_out, sems):
@@ -530,14 +536,15 @@
             pltpu.VMEM((group, halves, LANES), jnp.int32),
             pltpu.VMEM((-(-5 * tiles // 8) * 8, LANES), jnp.int32),
             pltpu.VMEM((rows + 1, LANES, 4 * LANES), BF16),
-            pltpu.VMEM((cap, 5 * tiles * LANES), BF16),
-            pltpu.VMEM((5 * tiles * LANES, cap), BF16),
-            pltpu.VMEM((group * cap, LANES), BF16),
+            pltpu.VMEM((cap, 5 * tiles * LANES), F8),
+            pltpu.VMEM((5 * tiles * LANES, cap), F8),
+            pltpu.VMEM((group * cap, LANES), F8),
             pltpu.VMEM((4, 16 * (rows + 1), LANES), F32),
             pltpu.VMEM((8 * (rows + 1), LANES), F32),
             pltpu.VMEM((6 * group, 5 * tiles * LANES), BF16),
             pltpu.VMEM((6 * rows, group * cap), BF16),
             pltpu.VMEM((group * cap, LANES), jnp.int32),
+            pltpu.VMEM((tiles, LANES, LANES), F32),
             pltpu.VMEM((group, 8, cap), F32),
             pltpu.VMEM((group, 8, cap), F32),
             pltpu.VMEM((STEPS - 1, group, 8, cap), F32),
@@ -546,21 +553,17 @@
             pltpu.VMEM((STEPS, group, 4, cap), F32),
             pltpu.VMEM((STEPS - 1, 3, LANES), F32),
             pltpu.VMEM((STEPS - 1, 3, LANES), F32),
-            pltpu.VMEM((STEPS, 3, LANES), F32),
-            pltpu.VMEM((STEPS, 3, LANES), F32),
+            pltpu.VMEM((STEPS, 2, 3, LANES), F32),
             pltpu.VMEM((4, LANES), jnp.int32),
             pltpu.VMEM((8, LANES), F32),
             pltpu.VMEM((2, LANES), F32),
             pltpu.VMEM((1, LANES), F32),
             pltpu.VMEM((3, LANES), F32),
-            dma((STEPS, group - 1)),
-            dma((STEPS, group)),
-            dma((STEPS, group - 1)),
-            dma((STEPS, group)),
+            dma((1,)),
+            dma((STEPS,)),
             dma((STEPS, 2)),
-            dma((STEPS, 2)),
-            dma((5,)),
-            dma((5,)),
+            dma((STEPS,)),
+            dma((1,)),
         ],
         compiler_params=pltpu.CompilerParams(
             collective_id=0, has_side_effects=True, vmem_limit_bytes=24 * 1024 * 1024

time: 29.6 us -> 28.1 us (0.949)
  Pallas kernels: 28 us -> 26.6 us
    pallas_call x1, Pallas kernels: 27.4 us -> 25.9 us  [per_device(): pl.pallas_call(functools.partial(kernel, sizes), out_shape=(state, state,...]
where the time goes in v3:
time: 28.1 us; the launch traced here: 27.9 us
  Pallas kernels  26.6 us (95%)
  between operations  1.29 us (5%)
    pallas_call x1, Pallas kernels, per_device(): pl.pallas_call(functools.partial(kernel, sizes), out_shape=(state, state,...  25.9 us
    pallas_call x1, Pallas kernels, per_device(): pl.pallas_call(put_out, out_shape=(state, state, state), in_specs=[vmem]...  0.65 us

profile of v3, /device:TPU:0, one launch (start us, length us, event | category | flops | bytes accessed | tf_op | source)
XLA Modules:
  0.0 27.9 jit_solution(2055171049846162890)
XLA Ops:
  1.3 25.9 %shard_map.148 = (f32[3,1024]{1,0:T(4,128)S(1)}, f32[3,1024]{1,0:T(4,128)S(1)}, f32[3,1024]{1,0:T(4,128)S(1)}) custom-call(f32[3,1024]{1,0:T(4,128)} %coords_hbm.1, f32[3,1024]{1,0:T(4,128)} %velocity_hbm.1, f32[8,128]{1,0:T(8,128)} %bitcast.2, s32[4,1024]{1,0:T(4,128)} %corner_hbm.1, f32[8,1024]{1,0:T(8,128)} %grad_hbm.1, f32[2,1024]{1,0:T(2,128)} %angles_hbm.1, ...), custom_call_target="tpu_custom_call" | custom-call | tf_op jit(solution)/shard_map/pallas_call | solution.py:523
  27.2 0.6 %shard_map.149 = (f32[3,1024]{1,0:T(4,128)}, f32[3,1024]{1,0:T(4,128)}, f32[3,1024]{1,0:T(4,128)}) custom-call(f32[3,1024]{1,0:T(4,128)S(1)} %get-tuple-element.6.coords_in, f32[3,1024]{1,0:T(4,128)S(1)} %get-tuple-element.7.velocity_in, f32[3,1024]{1,0:T(4,128)S(1)} %get-tuple-element.8.stress_in), custom_call_target="tpu_custom_call" | custom-call | tf_op jit(solution)/shard_map/pallas_call | solution.py:572

commit v4 on v3

--- a/solution.py
+++ b/solution.py
@@ -1,4 +1,5 @@
 import functools
+import math
 
 import jax
 import jax.numpy as jnp
@@ -52,7 +53,7 @@
     send_buf, recv_buf, again_buf, fresh_buf, back_buf, answer_buf,
     first_buf, last_buf, edge_recv,
     corner_prev, grad_prev, angles_prev, volume_prev, stress_prev,
-    send_sem, out_sem, back_sem, edge_sem, prev_sem,
+    send_sem, out_sem, back_sem, edge_sem,
 ):
     n_len, n_wid, n_dep = sizes
     group = n_wid * n_dep
@@ -89,20 +90,22 @@
     after = by_id(lax.rem(my_id + 1, devices))
 
     loads = [
-        pltpu.make_async_copy(src, dst, in_sem.at[n])
+        pltpu.make_async_copy(src, dst, in_sem.at[min(n, 4)])
         for n, (src, dst) in enumerate((
             (send_hbm, send_in), (velocity_hbm, velocity_in), (coords_hbm, coords_in),
-            (corner_hbm, corner_in), (stress_hbm, stress_in), (grad_hbm, grad_in),
+            (stress_hbm, stress_in), (corner_hbm, corner_in), (grad_hbm, grad_in),
             (angles_hbm, angles_in), (mass_hbm, mass_in), (volume_hbm, volume_in),
             (nodes_hbm, nodes_in), (facets_hbm, facets_in), (mask_hbm, mask_in),
         ))
     ]
+    for load in loads[:3]:
+        load.start()
     barrier = pltpu.get_barrier_semaphore()
     for wid, dep in peers:
         pl.semaphore_signal(barrier, inc=1, device_id=(my_len, wid, dep), device_id_type=MESH)
     pl.semaphore_signal(barrier, inc=1, device_id=before, device_id_type=MESH)
     pl.semaphore_signal(barrier, inc=1, device_id=after, device_id_type=MESH)
-    for load in loads:
+    for load in loads[3:]:
         load.start()
     for load in loads[:3]:
         load.wait()
@@ -169,7 +172,7 @@
             (volume_in.at[pl.ds(rows - 1, 1), :], volume_prev),
         )
         return [
-            remote(src, dst, prev_sem.at[0], after) for src, dst in pairs
+            remote(src, dst, edge_sem.at[STEPS], after) for src, dst in pairs
         ]
 
     far_count = n_dep * (n_wid // 2)
@@ -179,9 +182,9 @@
         if back:
             src, dst, depth, sem = back_buf.at[step], answer_buf.at[step], 3, back_sem.at[step, int(j < far_count)]
         elif step == 0:
-            src, dst, depth, sem = send_buf, recv_buf, 6, out_sem.at[step]
+            src, dst, depth, sem = send_buf, recv_buf, 6, out_sem.at[step, int(j < far_count)]
         else:
-            src, dst, depth, sem = again_buf.at[step - 1], fresh_buf.at[step - 1], 3, out_sem.at[step]
+            src, dst, depth, sem = again_buf.at[step - 1], fresh_buf.at[step - 1], 3, out_sem.at[step, int(j < far_count)]
         return remote(
             src.at[places[j], pl.ds(0, depth)], dst.at[my_place, pl.ds(0, depth)], sem, (my_len, wid, dep)
         )
@@ -216,8 +219,11 @@
             copy.start()
 
         if step == 0:
-            for load in loads[3:]:
-                load.wait()
+            loads[3].wait()
+            words = sum(math.prod(dst.shape) for dst in (
+                corner_in, grad_in, angles_in, mass_in, volume_in, nodes_in, facets_in, mask_in,
+            ))
+            drain(column_buf.at[pl.ds(0, words // LANES)], in_sem.at[4])
             for copy in prev_copies():
                 copy.start()
             for i in range(rows):
@@ -250,7 +256,7 @@
                 return (cos_p * cos_a, cos_p * sin_a, -sin_p), (-sin_a, cos_a)
 
             volume = volume_in[...]
-            mass = mass_in[...]
+            pace = TIME_STEP / mass_in[...]
             gx = [grad[pl.ds(a * rows, rows), :] for a in range(4)]
             gy = [grad[pl.ds((4 + a) * rows, rows), :] for a in range(4)]
             own = (frame(polar, azim), volume, gx, gy, corner_low, corner_far)
@@ -275,29 +281,31 @@
         mine, landed = (send_buf, recv_buf) if step == 0 else (again_buf.at[step - 1], fresh_buf.at[step - 1])
         landed[my_place] = mine[my_place]
         depth = 6 if step == 0 else 3
-        drain(landed.at[pl.ds(0, count), pl.ds(0, depth)], out_sem.at[step])
-        table = []
         deep = 16 if step == 0 else 8
-        for g in range(group):
-            first, second = split(landed[g])
-            if step == 0:
-                table += [first, second]
-            else:
-                table.append(jnp.where(eight_wide < 4, first, jnp.roll(second, 4, axis=0)))
-        table = jnp.concatenate(table, axis=0).astype(BF16)
-        state = []
-        for b in range(0, 5 * tiles, 2):
-            looked = nn_dot(table, look_hot[:, pl.ds(b * LANES, 2 * LANES)])
-            for side in range(2):
-                high = jnp.broadcast_to(slots_high[b + side : b + side + 1], (8, LANES))
-                block = looked[:, side * LANES : (side + 1) * LANES]
-                first, second = block[:8], block[deep - 8 : deep]
-                for g in range(1, group):
-                    match = high == g
-                    first = jnp.where(match, block[g * deep : g * deep + 8], first)
-                    if step == 0:
-                        second = jnp.where(match, block[g * deep + 8 : g * deep + 16], second)
-                state.append(first + (second if step == 0 else jnp.roll(first, 4, axis=0)))
+        taken = [[jnp.zeros((8, LANES), F32)] * (deep // 8) for b in range(5 * tiles)]
+        for far, base in ((0, bases[1]), (1, bases[0])):
+            landing = far_count if far else count - far_count
+            drain(landed.at[pl.ds(0, landing), pl.ds(0, depth)], out_sem.at[step, far])
+            table = []
+            for g in range(segment):
+                first, second = split(landed[base + g])
+                if step == 0:
+                    table += [first, second]
+                else:
+                    table.append(jnp.where(eight_wide < 4, first, jnp.roll(second, 4, axis=0)))
+            table = jnp.concatenate(table, axis=0).astype(BF16)
+            for b in range(0, 5 * tiles, 2):
+                looked = nn_dot(table, look_hot[:, pl.ds(b * LANES, 2 * LANES)])
+                for side in range(2):
+                    high = jnp.broadcast_to(slots_high[b + side : b + side + 1] - base, (8, LANES))
+                    block = looked[:, side * LANES : (side + 1) * LANES]
+                    for g in range(segment):
+                        match = high == g
+                        taken[b + side] = [
+                            jnp.where(match, block[g * deep + 8 * p : g * deep + 8 * p + 8], old)
+                            for p, old in enumerate(taken[b + side])
+                        ]
+        state = [t[0] + (t[1] if step == 0 else jnp.roll(t[0], 4, axis=0)) for t in taken]
         slots = jnp.zeros((6 * group, cap), F32)
         for pair in range(tiles // 2):
             pair_tiles = (2 * pair, 2 * pair + 1)
@@ -311,7 +319,31 @@
                     bodies[at] = jnp.where(eight < 3, bodies[at], moved)
             if step + 1 < STEPS:
                 old_bodies.update(bodies)
-            columns = jnp.transpose(jnp.concatenate([bodies[t, 0] for t in pair_tiles], axis=0))
+            tall, across_rows = [], [[] for _ in range(6)]
+            for t in pair_tiles:
+                high_part, rest = split(bodies[t, 0])
+                mid_part, low_part = split(rest)
+                tall.append(jnp.where(
+                    eight % 4 == 3, 1.0,
+                    jnp.where(eight < 3, jnp.roll(high_part, 5, axis=0), jnp.roll(mid_part, 1, axis=0)),
+                ))
+                tall.append(jnp.where(eight < 3, jnp.roll(low_part, 5, axis=0), jnp.where(eight == 3, 1.0, 0.0)))
+                high_part, rest = split(-bodies[t, 1])
+                mid_part, low_part = split(rest)
+                for k in range(3):
+                    unit = jnp.where(eight % 4 == k, 1.0, 0.0)
+                    spread = [jnp.broadcast_to(p[3 + k : 4 + k], (8, LANES)) for p in (high_part, mid_part, low_part)]
+                    block = [
+                        jnp.where(eight == 3, spread[0], jnp.where(eight == 7, spread[1], unit)),
+                        jnp.where(eight == 3, spread[2], jnp.where(eight < 3, unit, 0.0)),
+                    ]
+                    none = [jnp.zeros((8, LANES), F32)] * 2
+                    whole_block = block + none if t % 2 == 0 else none + block
+                    across_rows[3 * (t % 2) + k] = jnp.concatenate(whole_block, axis=0)
+            gaps = nn_dot(
+                jnp.transpose(jnp.concatenate(tall, axis=0)).astype(BF16),
+                jnp.concatenate(across_rows, axis=1).astype(BF16),
+            )
             for t in pair_tiles:
                 mixes = [
                     jnp.where(
@@ -323,9 +355,9 @@
                     jnp.concatenate(two_parts(jnp.where(eight == 3, 1.0, mix)), axis=0) for mix in mixes
                 ]
                 dist = jnp.zeros((LANES, LANES), F32)
-                for k in range(3, 6):
-                    at = 8 * (t % 2) + k
-                    gap = columns[:, at : at + 1] - bodies[t, 1][k : k + 1]
+                for k in range(3):
+                    at = (3 * (t % 2) + k) * LANES
+                    gap = gaps[:, at : at + LANES]
                     dist += gap * gap
                 w1, w2 = two_parts(weight_in[t] * jnp.maximum(RADIUS_SQ - dist, 0.0))
                 to_facet = nn_dot(
@@ -356,7 +388,7 @@
             group_copy(step, j, True).start()
 
         if step == 0:
-            drain(force_rows.at[pl.ds(0, 18)], prev_sem.at[0])
+            drain(force_rows.at[pl.ds(0, 18)], edge_sem.at[STEPS])
 
             def whole(row):
                 return jnp.broadcast_to(row, (8, LANES))
@@ -480,9 +512,7 @@
             summed = nn_dot(pairs[:, at], node_hot[at, :])
             contact += summed[: 3 * rows] + summed[3 * rows :]
         for k in range(3):
-            fresh = velocity_rows(k) + TIME_STEP * (
-                internal[k] + contact[k * rows : (k + 1) * rows]
-            ) / mass
+            fresh = velocity_rows(k) + pace * (internal[k] + contact[k * rows : (k + 1) * rows])
             vel[pl.ds(k * 2 * rows, rows), :] = fresh
             pos[pl.ds(k * rows, rows), :] = pos[pl.ds(k * rows, rows), :] + TIME_STEP * fresh
 
@@ -526,7 +556,7 @@
         in_specs=[hbm] * 12 + [pl.BlockSpec(memory_space=pltpu.SMEM)],
         out_specs=(vmem, vmem, vmem),
         scratch_shapes=[pltpu.VMEM(a.shape, a.dtype) for a in arrays] + [
-            dma((len(arrays),)),
+            dma((5,)),
             pltpu.VMEM((3 * rows, LANES), F32),
             pltpu.VMEM((6 * rows, LANES), F32),
             pltpu.VMEM((4 * rows, LANES), jnp.int32),
@@ -560,10 +590,9 @@
             pltpu.VMEM((1, LANES), F32),
             pltpu.VMEM((3, LANES), F32),
             dma((1,)),
-            dma((STEPS,)),
             dma((STEPS, 2)),
-            dma((STEPS,)),
-            dma((1,)),
+            dma((STEPS, 2)),
+            dma((STEPS + 1,)),
         ],
         compiler_params=pltpu.CompilerParams(
             collective_id=0, has_side_effects=True, vmem_limit_bytes=24 * 1024 * 1024

time: 28.1 us -> 27.9 us (level)
  Pallas kernels: 26.6 us -> 26.3 us
where the time goes in v4:
time: 27.9 us; the launch traced here: 27.6 us
  Pallas kernels  26.3 us (94%)
  between operations  1.29 us (5%)
    pallas_call x1, Pallas kernels, per_device(): pl.pallas_call(functools.partial(kernel, sizes), out_shape=(state, state,...  25.7 us
    pallas_call x1, Pallas kernels, per_device(): pl.pallas_call(put_out, out_shape=(state, state, state), in_specs=[vmem]...  0.65 us

profile of v4, /device:TPU:0, one launch (start us, length us, event | category | flops | bytes accessed | tf_op | source)
XLA Modules:
  0.0 27.6 jit_solution(2970374011663705362)
XLA Ops:
  1.3 25.7 %shard_map.148 = (f32[3,1024]{1,0:T(4,128)S(1)}, f32[3,1024]{1,0:T(4,128)S(1)}, f32[3,1024]{1,0:T(4,128)S(1)}) custom-call(f32[3,1024]{1,0:T(4,128)} %coords_hbm.1, f32[3,1024]{1,0:T(4,128)} %velocity_hbm.1, f32[8,128]{1,0:T(8,128)} %bitcast.2, s32[4,1024]{1,0:T(4,128)} %corner_hbm.1, f32[8,1024]{1,0:T(8,128)} %grad_hbm.1, f32[2,1024]{1,0:T(2,128)} %angles_hbm.1, ...), custom_call_target="tpu_custom_call" | custom-call | tf_op jit(solution)/shard_map/pallas_call | solution.py:553
  26.9 0.6 %shard_map.149 = (f32[3,1024]{1,0:T(4,128)}, f32[3,1024]{1,0:T(4,128)}, f32[3,1024]{1,0:T(4,128)}) custom-call(f32[3,1024]{1,0:T(4,128)S(1)} %get-tuple-element.6.coords_in, f32[3,1024]{1,0:T(4,128)S(1)} %get-tuple-element.7.velocity_in, f32[3,1024]{1,0:T(4,128)S(1)} %get-tuple-element.8.stress_in), custom_call_target="tpu_custom_call" | custom-call | tf_op jit(solution)/shard_map/pallas_call | solution.py:601

commit v5 on v4

--- a/solution.py
+++ b/solution.py
@@ -239,7 +239,6 @@
                     tile_ids[pl.ds(5 * t + 1 + a, 1), :] = facets_in[a, pl.ds(t, 1), :]
                 live = jnp.where(t < count_in[0], 1.0, 0.0)
                 weight_in[t] = mask_in[t].astype(F32) * live
-            old_bodies = {}
             first_row = lax.broadcasted_iota(jnp.int32, (rows, LANES), 0) * LANES
             corner_low, corner_far = [], []
             for a in range(4):
@@ -307,80 +306,79 @@
                         ]
         state = [t[0] + (t[1] if step == 0 else jnp.roll(t[0], 4, axis=0)) for t in taken]
         slots = jnp.zeros((6 * group, cap), F32)
-        for pair in range(tiles // 2):
-            pair_tiles = (2 * pair, 2 * pair + 1)
-            bodies = {}
-            for t in pair_tiles:
-                bodies[t, 0] = state[5 * t]
-                bodies[t, 1] = 0.25 * sum(state[5 * t + 1 + a] for a in range(4))
-            if step:
-                for at in bodies:
-                    moved = old_bodies[at] + TIME_STEP * jnp.roll(bodies[at], 3, axis=0)
-                    bodies[at] = jnp.where(eight < 3, bodies[at], moved)
-            if step + 1 < STEPS:
-                old_bodies.update(bodies)
-            tall, across_rows = [], [[] for _ in range(6)]
-            for t in pair_tiles:
-                high_part, rest = split(bodies[t, 0])
-                mid_part, low_part = split(rest)
-                tall.append(jnp.where(
-                    eight % 4 == 3, 1.0,
-                    jnp.where(eight < 3, jnp.roll(high_part, 5, axis=0), jnp.roll(mid_part, 1, axis=0)),
-                ))
-                tall.append(jnp.where(eight < 3, jnp.roll(low_part, 5, axis=0), jnp.where(eight == 3, 1.0, 0.0)))
-                high_part, rest = split(-bodies[t, 1])
-                mid_part, low_part = split(rest)
-                for k in range(3):
-                    unit = jnp.where(eight % 4 == k, 1.0, 0.0)
-                    spread = [jnp.broadcast_to(p[3 + k : 4 + k], (8, LANES)) for p in (high_part, mid_part, low_part)]
-                    block = [
-                        jnp.where(eight == 3, spread[0], jnp.where(eight == 7, spread[1], unit)),
-                        jnp.where(eight == 3, spread[2], jnp.where(eight < 3, unit, 0.0)),
-                    ]
-                    none = [jnp.zeros((8, LANES), F32)] * 2
-                    whole_block = block + none if t % 2 == 0 else none + block
-                    across_rows[3 * (t % 2) + k] = jnp.concatenate(whole_block, axis=0)
-            gaps = nn_dot(
-                jnp.transpose(jnp.concatenate(tall, axis=0)).astype(BF16),
-                jnp.concatenate(across_rows, axis=1).astype(BF16),
+        bodies = {}
+        for t in range(tiles):
+            bodies[t, 0] = state[5 * t]
+            bodies[t, 1] = 0.25 * sum(state[5 * t + 1 + a] for a in range(4))
+        if step:
+            for at in bodies:
+                moved = old_bodies[at] + TIME_STEP * jnp.roll(bodies[at], 3, axis=0)
+                bodies[at] = jnp.where(eight < 3, bodies[at], moved)
+        old_bodies = bodies
+        tall, blocks_wide = [], []
+        for t in range(tiles):
+            high_part, rest = split(bodies[t, 0])
+            mid_part, low_part = split(rest)
+            tall.append(jnp.where(
+                eight % 4 == 3, 1.0,
+                jnp.where(eight < 3, jnp.roll(high_part, 5, axis=0), jnp.roll(mid_part, 1, axis=0)),
+            ))
+            tall.append(jnp.where(eight < 3, jnp.roll(low_part, 5, axis=0), jnp.where(eight == 3, 1.0, 0.0)))
+            high_part, rest = split(-bodies[t, 1])
+            mid_part, low_part = split(rest)
+            for k in range(3):
+                unit = jnp.where(eight % 4 == k, 1.0, 0.0)
+                spread = [jnp.broadcast_to(p[3 + k : 4 + k], (8, LANES)) for p in (high_part, mid_part, low_part)]
+                block = [
+                    jnp.where(eight == 3, spread[0], jnp.where(eight == 7, spread[1], unit)),
+                    jnp.where(eight == 3, spread[2], jnp.where(eight < 3, unit, 0.0)),
+                ]
+                none = [jnp.zeros((16, LANES), F32)]
+                blocks_wide.append(jnp.concatenate(none * t + block + none * (tiles - 1 - t), axis=0))
+        gaps = nn_dot(
+            jnp.transpose(jnp.concatenate(tall, axis=0)).astype(BF16),
+            jnp.concatenate(blocks_wide, axis=1).astype(BF16),
+        )
+        dots = []
+        for t in range(tiles):
+            mixes = [
+                jnp.where(
+                    eight < 3, STIFFNESS * jnp.roll(bodies[t, s], 5, axis=0) - DAMPING * bodies[t, s], 0.0
+                )
+                for s in range(2)
+            ]
+            left_a, left_b = [
+                jnp.concatenate(two_parts(jnp.where(eight == 3, 1.0, mix)), axis=0) for mix in mixes
+            ]
+            dist = jnp.zeros((LANES, LANES), F32)
+            for k in range(3):
+                at = (3 * t + k) * LANES
+                gap = gaps[:, at : at + LANES]
+                dist += gap * gap
+            w1, w2 = two_parts(weight_in[t] * jnp.maximum(RADIUS_SQ - dist, 0.0))
+            to_facet = nn_dot(
+                jnp.concatenate([left_a, left_a], axis=1), jnp.concatenate([w1, w2], axis=0)
             )
-            for t in pair_tiles:
-                mixes = [
-                    jnp.where(
-                        eight < 3, STIFFNESS * jnp.roll(bodies[t, s], 5, axis=0) - DAMPING * bodies[t, s], 0.0
-                    )
-                    for s in range(2)
-                ]
-                left_a, left_b = [
-                    jnp.concatenate(two_parts(jnp.where(eight == 3, 1.0, mix)), axis=0) for mix in mixes
-                ]
-                dist = jnp.zeros((LANES, LANES), F32)
-                for k in range(3):
-                    at = (3 * (t % 2) + k) * LANES
-                    gap = gaps[:, at : at + LANES]
-                    dist += gap * gap
-                w1, w2 = two_parts(weight_in[t] * jnp.maximum(RADIUS_SQ - dist, 0.0))
-                to_facet = nn_dot(
-                    jnp.concatenate([left_a, left_a], axis=1), jnp.concatenate([w1, w2], axis=0)
-                )
-                to_node = nt_dot(
-                    jnp.concatenate([left_b, left_b], axis=1), jnp.concatenate([w1, w2], axis=1)
-                )
-                to_facet = to_facet[:8] + to_facet[8:]
-                to_node = to_node[:8] + to_node[8:]
-                node_force = mixes[0] * to_node[3:4] - to_node
-                facet_force = -0.25 * (to_facet - to_facet[3:4] * mixes[1])
-                for force, blocks in ((node_force, [5 * t]), (facet_force, [5 * t + 1 + a for a in range(4)])):
-                    matches = [group_iota == slots_high[b : b + 1] for b in blocks]
-                    for part, value in enumerate(split(force)):
-                        for k in range(3):
-                            row = jnp.broadcast_to(value[k : k + 1], (group, LANES))
-                            for b, match in zip(blocks, matches):
-                                tile_lhs[pl.ds((part * 3 + k) * group, group), pl.ds(b * LANES, LANES)] = (
-                                    jnp.where(match, row, 0.0).astype(BF16)
-                                )
-            at = pl.ds(pair * 10 * LANES, 10 * LANES)
-            slots += nn_dot(tile_lhs[:, at], slot_hot[at, :])
+            to_node = nt_dot(
+                jnp.concatenate([left_b, left_b], axis=1), jnp.concatenate([w1, w2], axis=1)
+            )
+            dots.append((mixes, to_facet, to_node))
+        for t in range(tiles):
+            mixes, to_facet, to_node = dots[t]
+            to_facet = to_facet[:8] + to_facet[8:]
+            to_node = to_node[:8] + to_node[8:]
+            node_force = mixes[0] * to_node[3:4] - to_node
+            facet_force = -0.25 * (to_facet - to_facet[3:4] * mixes[1])
+            for force, blocks in ((node_force, [5 * t]), (facet_force, [5 * t + 1 + a for a in range(4)])):
+                matches = [group_iota == slots_high[b : b + 1] for b in blocks]
+                for part, value in enumerate(split(force)):
+                    for k in range(3):
+                        row = jnp.broadcast_to(value[k : k + 1], (group, LANES))
+                        for b, match in zip(blocks, matches):
+                            tile_lhs[pl.ds((part * 3 + k) * group, group), pl.ds(b * LANES, LANES)] = (
+                                jnp.where(match, row, 0.0).astype(BF16)
+                            )
+        slots = nn_dot(tile_lhs[...], slot_hot[...])
         slots = slots[: 3 * group] + slots[3 * group :]
         for k in range(3):
             back_buf[step, :, k, :] = slots[k * group : (k + 1) * group]

time: 27.9 us -> 27.5 us (0.986)
  Pallas kernels: 26.3 us -> 25.9 us
    pallas_call x1, Pallas kernels: 25.7 us -> 25.3 us  [per_device(): pl.pallas_call(functools.partial(kernel, sizes), out_shape=(state, state,...]
where the time goes in v5:
time: 27.5 us; the launch traced here: 27.2 us
  Pallas kernels  25.9 us (94%)
  between operations  1.29 us (5%)
    pallas_call x1, Pallas kernels, per_device(): pl.pallas_call(functools.partial(kernel, sizes), out_shape=(state, state,...  25.3 us
    pallas_call x1, Pallas kernels, per_device(): pl.pallas_call(put_out, out_shape=(state, state, state), in_specs=[vmem]...  0.65 us

profile of v5, /device:TPU:0, one launch (start us, length us, event | category | flops | bytes accessed | tf_op | source)
XLA Modules:
  0.0 27.2 jit_solution(9492092884354672253)
XLA Ops:
  1.3 25.3 %shard_map.148 = (f32[3,1024]{1,0:T(4,128)S(1)}, f32[3,1024]{1,0:T(4,128)S(1)}, f32[3,1024]{1,0:T(4,128)S(1)}) custom-call(f32[3,1024]{1,0:T(4,128)} %coords_hbm.1, f32[3,1024]{1,0:T(4,128)} %velocity_hbm.1, f32[8,128]{1,0:T(8,128)} %bitcast.2, s32[4,1024]{1,0:T(4,128)} %corner_hbm.1, f32[8,1024]{1,0:T(8,128)} %grad_hbm.1, f32[2,1024]{1,0:T(2,128)} %angles_hbm.1, ...), custom_call_target="tpu_custom_call" | custom-call | tf_op jit(solution)/shard_map/pallas_call | solution.py:551
  26.5 0.6 %shard_map.149 = (f32[3,1024]{1,0:T(4,128)}, f32[3,1024]{1,0:T(4,128)}, f32[3,1024]{1,0:T(4,128)}) custom-call(f32[3,1024]{1,0:T(4,128)S(1)} %get-tuple-element.6.coords_in, f32[3,1024]{1,0:T(4,128)S(1)} %get-tuple-element.7.velocity_in, f32[3,1024]{1,0:T(4,128)S(1)} %get-tuple-element.8.stress_in), custom_call_target="tpu_custom_call" | custom-call | tf_op jit(solution)/shard_map/pallas_call | solution.py:599

commit v6 on v5

--- a/solution.py
+++ b/solution.py
@@ -180,11 +180,11 @@
     def group_copy(step, j, back):
         wid, dep = peers[j]
         if back:
-            src, dst, depth, sem = back_buf.at[step], answer_buf.at[step], 3, back_sem.at[step, int(j < far_count)]
+            src, dst, depth, sem = back_buf.at[step], answer_buf.at[step], 3, back_sem.at[0, int(j < far_count)]
         elif step == 0:
-            src, dst, depth, sem = send_buf, recv_buf, 6, out_sem.at[step, int(j < far_count)]
+            src, dst, depth, sem = send_buf, recv_buf, 6, out_sem.at[0, int(j < far_count)]
         else:
-            src, dst, depth, sem = again_buf.at[step - 1], fresh_buf.at[step - 1], 3, out_sem.at[step, int(j < far_count)]
+            src, dst, depth, sem = again_buf.at[step - 1], fresh_buf.at[step - 1], 3, out_sem.at[0, int(j < far_count)]
         return remote(
             src.at[places[j], pl.ds(0, depth)], dst.at[my_place, pl.ds(0, depth)], sem, (my_len, wid, dep)
         )
@@ -284,7 +284,7 @@
         taken = [[jnp.zeros((8, LANES), F32)] * (deep // 8) for b in range(5 * tiles)]
         for far, base in ((0, bases[1]), (1, bases[0])):
             landing = far_count if far else count - far_count
-            drain(landed.at[pl.ds(0, landing), pl.ds(0, depth)], out_sem.at[step, far])
+            drain(landed.at[pl.ds(0, landing), pl.ds(0, depth)], out_sem.at[0, far])
             table = []
             for g in range(segment):
                 first, second = split(landed[base + g])
@@ -493,7 +493,7 @@
         contact = jnp.zeros((3 * rows, LANES), F32)
         for begin in range(0, group, batch):
             answers = batch - 1 if begin == 0 else batch
-            drain(answer_buf.at[step, pl.ds(0, answers), pl.ds(0, 3)], back_sem.at[step, int(begin > 0)])
+            drain(answer_buf.at[step, pl.ds(0, answers), pl.ds(0, 3)], back_sem.at[0, int(begin > 0)])
             for n in range(begin, begin + batch):
                 g = arrival[n]
                 source = answer_buf if n else back_buf
@@ -588,8 +588,8 @@
             pltpu.VMEM((1, LANES), F32),
             pltpu.VMEM((3, LANES), F32),
             dma((1,)),
-            dma((STEPS, 2)),
-            dma((STEPS, 2)),
+            dma((1, 2)),
+            dma((1, 2)),
             dma((STEPS + 1,)),
         ],
         compiler_params=pltpu.CompilerParams(

time: 27.5 us -> 27.4 us (level)
  no operation moved by 1% of the time
where the time goes in v6:
time: 27.4 us; the launch traced here: 27.2 us
  Pallas kernels  25.9 us (95%)
  between operations  1.29 us (5%)
    pallas_call x1, Pallas kernels, per_device(): pl.pallas_call(functools.partial(kernel, sizes), out_shape=(state, state,...  25.2 us
    pallas_call x1, Pallas kernels, per_device(): pl.pallas_call(put_out, out_shape=(state, state, state), in_specs=[vmem]...  0.65 us

profile of v6, /device:TPU:0, one launch (start us, length us, event | category | flops | bytes accessed | tf_op | source)
XLA Modules:
  0.0 27.2 jit_solution(9091719297422391322)
XLA Ops:
  1.3 25.2 %shard_map.148 = (f32[3,1024]{1,0:T(4,128)S(1)}, f32[3,1024]{1,0:T(4,128)S(1)}, f32[3,1024]{1,0:T(4,128)S(1)}) custom-call(f32[3,1024]{1,0:T(4,128)} %coords_hbm.1, f32[3,1024]{1,0:T(4,128)} %velocity_hbm.1, f32[8,128]{1,0:T(8,128)} %bitcast.2, s32[4,1024]{1,0:T(4,128)} %corner_hbm.1, f32[8,1024]{1,0:T(8,128)} %grad_hbm.1, f32[2,1024]{1,0:T(2,128)} %angles_hbm.1, ...), custom_call_target="tpu_custom_call" | custom-call | tf_op jit(solution)/shard_map/pallas_call | solution.py:551
  26.5 0.6 %shard_map.149 = (f32[3,1024]{1,0:T(4,128)}, f32[3,1024]{1,0:T(4,128)}, f32[3,1024]{1,0:T(4,128)}) custom-call(f32[3,1024]{1,0:T(4,128)S(1)} %get-tuple-element.6.coords_in, f32[3,1024]{1,0:T(4,128)S(1)} %get-tuple-element.7.velocity_in, f32[3,1024]{1,0:T(4,128)S(1)} %get-tuple-element.8.stress_in), custom_call_target="tpu_custom_call" | custom-call | tf_op jit(solution)/shard_map/pallas_call | solution.py:599
